TPU v7x, 32 devices: a whole 2x2x4 slice. The times are simulated.
32 devices in a mesh: sample: 4 (over y, x), gz: 8 (over z, core).
Axes of the slice: x: 2, y: 2, z: 4, core: 2. Of those that a mesh axis runs over, the one named last changes fastest.
Arguments:
- field_now: float32 [12, 16, 160, 256], P('sample', 'gz'), parts along dimension 0, may hold values from -6 to 6
- field_before: float32 [12, 16, 160, 256], P('sample', 'gz'), parts along dimension 0, may hold values from -6 to 6
- lame_lambda: float32 [16, 640, 256], P('gz', 'sample'), parts along dimension 1, may hold values from 0.5 to 1.5
- shear_modulus: float32 [16, 640, 256], P('gz', 'sample'), parts along dimension 1, may hold values from 0.5 to 1.5
- density: float32 [16, 640, 256], P('gz', 'sample'), parts along dimension 1, may hold values from 1 to 2
- source_field: float32 [12, 16, 160, 256], P('sample', 'gz'), parts along dimension 0, may hold values from -6 to 6
- wavelet: float32 [32], P('sample'), parts along dimension 0, may hold values from -4 to 4
- prior_mean: float32 [16, 640, 256], P('gz', 'sample'), parts along dimension 1, may hold values from 0.5 to 1.5
- steps_taken: float32 [16, 16, 160, 256], P('sample', 'gz'), parts along dimension 0
- grad_change: float32 [16, 16, 160, 256], P('sample', 'gz'), parts along dimension 0, as said below
Outputs:
- field_final: float32 [12, 16, 160, 256], P('sample', 'gz'), parts along dimension 0
- gradient: float32 [16, 640, 256], P('gz', 'sample'), parts along dimension 1
- direction: float32 [16, 640, 256], P('gz', 'sample'), parts along dimension 1
There are 4 independent parts, one for each index of `sample`. A program takes and returns all parts, laid end to end along the dimension named above; each array names one. Nothing has to cross between parts.
Inputs may be any that keep to these rules, and one draw needn't show every extreme that they name: Each entry of grad_change is 0.5 to 2 times the matching entry of steps_taken.
All inputs are finite; a program needn't handle non-finite values.
Results may differ from a plain program's by a relative error of at most 0.0003.
Values sent between devices are 32-bit elements; how exact they have to be, the bound alone decides.
A program may use at most 64 MiB of HBM per device.

v0:
```python
import functools

import jax
import jax.numpy as jnp
from jax import lax
from jax.experimental import pallas as pl
from jax.experimental.pallas import tpu as pltpu
from jax.sharding import PartitionSpec as P

PAD = 8
CHUNK_ROWS = 16


def chunk_rows(rows):
    size = CHUNK_ROWS
    while rows % size:
        size //= 2
    return size


def tile(start):
    return pl.ds(pl.multiple_of(start, 8), 8)


def kernel(
    n,
    steps,
    pairs,
    size,
    now_hbm,
    before_hbm,
    lame_hbm,
    shear_hbm,
    density_hbm,
    source_hbm,
    wavelet,
    prior_hbm,
    taken_hbm,
    change_hbm,
    final_hbm,
    grad,
    direction,
    even,
    odd,
    lame,
    shear,
    coeff,
    source,
    prior,
    taken,
    change,
    sums,
    part,
    gathered,
    load_sem,
    store_sem,
    send_sem,
    recv_sem,
    part_send,
    part_recv,
):
    me = lax.axis_index("gz")
    rows, cols = lame.shape[1], lame.shape[2]
    chunks = rows // size
    tiles = size // 8
    has_low = me > 0
    has_high = me < n - 1
    inside = pl.ds(PAD, rows)

    loads = [
        pltpu.make_async_copy(src, dst, load_sem.at[i])
        for i, (src, dst) in enumerate(
            (
                (now_hbm, even.at[:, pl.ds(1, 2), inside]),
                (lame_hbm, lame),
                (shear_hbm, shear),
                (density_hbm, coeff),
                (before_hbm, odd.at[:, pl.ds(1, 2), inside]),
                (source_hbm, source),
                (taken_hbm, taken),
                (change_hbm, change),
                (prior_hbm, prior),
            )
        )
    ]
    for load in loads:
        load.start()

    barrier = pltpu.get_barrier_semaphore()
    for k in range(1, n):
        pl.semaphore_signal(
            barrier,
            inc=1,
            device_id={"gz": lax.rem(me + k, n)},
            device_id_type=pl.DeviceIdType.MESH,
        )

    edge = jnp.zeros((even.shape[0], 4, PAD, cols), jnp.float32)
    for ref in (even, odd):
        ref[:, :, pl.ds(0, PAD)] = edge
        ref[:, :, pl.ds(PAD + rows, PAD)] = edge

    def clear(plane):
        def body(t, carry):
            for ref in (even, odd):
                for comp in range(3):
                    ref[comp, plane, tile(PAD + 8 * t)] = jnp.zeros((8, cols), jnp.float32)
            return carry

        lax.fori_loop(0, rows // 8, body, 0)

    @pl.when(me == 0)
    def _():
        clear(0)

    @pl.when(me == n - 1)
    def _():
        clear(3)

    def rdma(ref, parity, up, chunk):
        where = pl.ds(pl.multiple_of(PAD + chunk * size, 8), size)
        side = 0 if up else 1
        target = lax.rem(me + (1 if up else n - 1), n)
        return pltpu.make_async_remote_copy(
            src_ref=ref.at[:, 2 if up else 1, where],
            dst_ref=ref.at[:, 0 if up else 3, where],
            send_sem=send_sem.at[parity, side, chunk],
            recv_sem=recv_sem.at[parity, side, chunk],
            device_id={"gz": target},
            device_id_type=pl.DeviceIdType.MESH,
        )

    def send(ref, parity, chunk):
        @pl.when(has_high)
        def _():
            rdma(ref, parity, True, chunk).start()

        @pl.when(has_low)
        def _():
            rdma(ref, parity, False, chunk).start()

    def sent(ref, parity, chunk):
        @pl.when(has_high)
        def _():
            rdma(ref, parity, True, chunk).wait_send()

        @pl.when(has_low)
        def _():
            rdma(ref, parity, False, chunk).wait_send()

    def received(ref, parity, chunk):
        @pl.when(has_low)
        def _():
            rdma(ref, parity, True, chunk).wait_recv()

        @pl.when(has_high)
        def _():
            rdma(ref, parity, False, chunk).wait_recv()

    loads[0].wait()
    pl.semaphore_wait(barrier, n - 1)

    def first(chunk, carry):
        send(even, 0, chunk)
        return carry

    lax.fori_loop(0, chunks, first, 0)

    for load in loads[1:4]:
        load.wait()

    def prepare(t, carry):
        for plane in range(2):
            at = (plane, tile(8 * t))
            lame[at] = lame[at] + shear[at]
            coeff[at] = 0.04 / coeff[at]
            grad[at] = jnp.zeros((8, cols), jnp.float32)
        return carry

    lax.fori_loop(0, rows // 8, prepare, 0)
    for load in loads[4:]:
        load.wait()

    half = cols // 2
    products = [(i, pairs + j) for i in range(pairs) for j in range(pairs)]
    products += [(pairs + i, pairs + j) for i in range(pairs) for j in range(i, pairs)]
    count = len(products)
    where_of = {pair: k for k, pair in enumerate(products)}
    for i in range(2 * pairs):
        where_of[(i, 2 * pairs)] = count + i

    def fold(value):
        out = value[:, 0:128]
        for k in range(1, cols // 128):
            out = out + value[:, 128 * k : 128 * (k + 1)]
        return out

    def stored(t, totals):
        totals = list(totals)
        for plane in range(2):
            vectors = [taken[i, plane, tile(8 * t)] for i in range(pairs)]
            vectors += [change[i, plane, tile(8 * t)] for i in range(pairs)]
            for k, (a, b) in enumerate(products):
                totals[k] = totals[k] + fold(vectors[a] * vectors[b])
        return tuple(totals)

    totals = lax.fori_loop(
        0, rows // 8, stored, tuple(jnp.zeros((8, 128), jnp.float32) for _ in products)
    )
    place = lax.broadcasted_iota(jnp.int32, (1, 128), 1)

    def whole(value):
        return jnp.sum(jnp.sum(value, axis=0, keepdims=True), axis=1, keepdims=True)

    line = jnp.zeros((1, 128), jnp.float32)
    for k in range(count):
        line = jnp.where(place == k, whole(totals[k]), line)
    part[...] = line
    for i in range(2 * pairs):
        sums[i] = jnp.zeros((8, 128), jnp.float32)

    row_at = lax.broadcasted_iota(jnp.int32, (8, cols), 0)
    col_at = lax.broadcasted_iota(jnp.int32, (8, cols), 1)
    is_top, is_bottom = row_at == 0, row_at == 7
    is_left, is_right = col_at == 0, col_at == cols - 1

    def along_x(previous, value, following):
        minus = pltpu.roll(jnp.where(is_bottom, previous, value), 1, 0)
        plus = pltpu.roll(jnp.where(is_top, following, value), 7, 0)
        return minus, plus

    def along_y(value):
        minus = jnp.where(is_left, 0.0, pltpu.roll(value, 1, 1))
        plus = jnp.where(is_right, 0.0, pltpu.roll(value, cols - 1, 1))
        return minus, plus

    def delta_y(value):
        minus, plus = along_y(value)
        return plus - minus

    def update(step, current, other, t):
        amplitude = wavelet[step]

        def load(comp, plane, shift=0):
            return current[comp, plane, tile(PAD + 8 * (t + shift))]

        for plane in range(2):
            low, mid, high = plane, plane + 1, plane + 2
            at = tile(8 * t)
            here = tile(PAD + 8 * t)

            def delta_z(comp, shift=0):
                return load(comp, high, shift) - load(comp, low, shift)

            def delta_xz(comp, centre):
                minus, plus = along_x(delta_z(comp, -1), centre, delta_z(comp, 1))
                return plus - minus

            centre = [load(comp, mid) for comp in range(3)]
            diff = [delta_z(comp) for comp in range(3)]
            total = [load(comp, high) + load(comp, low) for comp in range(3)]
            xs = [along_x(load(comp, mid, -1), centre[comp], load(comp, mid, 1)) for comp in range(3)]
            ys = [along_y(centre[comp]) for comp in range(3)]
            sum_x = [minus + plus for minus, plus in xs]
            sum_y = [minus + plus for minus, plus in ys]
            dx = [plus - minus for minus, plus in xs]
            lap = [
                (total[comp] + sum_x[comp]) + (sum_y[comp] - 6.0 * centre[comp])
                for comp in range(3)
            ]
            mixed = [
                delta_xz(1, diff[1]) + delta_y(diff[2]),
                delta_xz(0, diff[0]) + delta_y(dx[2]),
                delta_y(diff[0] + dx[1]),
            ]
            own = [total[0], sum_x[1], sum_y[2]]
            both = lame[plane, at]
            mu = shear[plane, at]
            rate = coeff[plane, at]
            grad[plane, at] = grad[plane, at] + (
                centre[0] * lap[0] + centre[1] * lap[1] + centre[2] * lap[2]
            )
            for comp in range(3):
                doubled = 2.0 * centre[comp]
                elastic = both * ((own[comp] - doubled) + 0.25 * mixed[comp]) + mu * lap[comp]
                other[comp, mid, here] = (
                    doubled
                    - other[comp, mid, here]
                    + rate * (elastic + amplitude * source[comp, plane, at])
                )

    def finish(t, totals):
        totals = list(totals)
        for plane in range(2):
            at = (plane, tile(8 * t))
            value = (shear[at] - prior[at]) + 0.02 * grad[at]
            grad[at] = value
            for i in range(pairs):
                totals[i] = totals[i] + fold(taken[(i,) + at] * value)
                totals[pairs + i] = totals[pairs + i] + fold(change[(i,) + at] * value)
        return tuple(totals)

    def advance(step, current, other, parity):
        received(current, parity, 0)

        def chunk_body(chunk, carry):
            @pl.when(chunk + 1 < chunks)
            def _():
                received(current, parity, chunk + 1)

            @pl.when(step > 0)
            def _():
                sent(other, 1 - parity, chunk)

            def tile_body(t, inner):
                update(step, current, other, chunk * tiles + t)
                return inner

            lax.fori_loop(0, tiles, tile_body, 0)

            @pl.when(step < steps - 1)
            def _():
                send(other, 1 - parity, chunk)

            if parity == 1:

                @pl.when(step == steps - 1)
                def _():
                    totals = lax.fori_loop(
                        chunk * tiles,
                        chunk * tiles + tiles,
                        finish,
                        tuple(sums[i] for i in range(2 * pairs)),
                    )
                    for i in range(2 * pairs):
                        sums[i] = totals[i]

            return carry

        lax.fori_loop(0, chunks, chunk_body, 0)

    def two_steps(k, carry):
        advance(2 * k, even, odd, 0)
        advance(2 * k + 1, odd, even, 1)
        return carry

    lax.fori_loop(0, steps // 2, two_steps, 0)

    line = part[...]
    for i in range(2 * pairs):
        line = jnp.where(place == count + i, whole(sums[i]), line)
    part[...] = line

    out = pltpu.make_async_copy(even.at[:, pl.ds(1, 2), inside], final_hbm, store_sem.at[0])
    exchange = [
        pltpu.make_async_remote_copy(
            src_ref=part,
            dst_ref=gathered.at[k - 1],
            send_sem=part_send.at[k - 1],
            recv_sem=part_recv.at[k - 1],
            device_id={"gz": lax.rem(me + k, n)},
            device_id_type=pl.DeviceIdType.MESH,
        )
        for k in range(1, n)
    ]
    for copy in exchange:
        copy.start()
    out.start()

    def last_sent(chunk, carry):
        sent(odd, 1, chunk)
        return carry

    lax.fori_loop(0, chunks, last_sent, 0)
    for copy in exchange:
        copy.wait_recv()
    line = part[...]
    for k in range(n - 1):
        line = line + gathered[k]

    def product(a, b):
        k = where_of[(min(a, b), max(a, b))]
        return jnp.sum(jnp.where(place == k, line, 0.0), axis=1, keepdims=True)

    cache = {}

    def inner(a, b):
        key = (min(a, b), max(a, b))
        if key not in cache:
            cache[key] = product(*key)
        return cache[key]

    gradient_at = 2 * pairs
    curvature = [inner(i, pairs + i) for i in range(pairs)]
    alphas = [None] * pairs
    for i in reversed(range(pairs)):
        value = inner(i, gradient_at)
        for j in range(i + 1, pairs):
            value = value - alphas[j] * inner(i, pairs + j)
        alphas[i] = value / curvature[i]
    newest = 2 * pairs - 1
    gamma = curvature[pairs - 1] / inner(newest, newest)
    changes = [-gamma * alphas[i] for i in range(pairs)]
    steps_coef = [None] * pairs
    for i in range(pairs):
        value = gamma * inner(pairs + i, gradient_at)
        for j in range(pairs):
            value = value + changes[j] * inner(pairs + i, pairs + j)
        for j in range(i):
            value = value + steps_coef[j] * inner(j, pairs + i)
        steps_coef[i] = alphas[i] - value / curvature[i]

    def spread(value):
        return -jnp.broadcast_to(value, (8, cols))

    by_grad = spread(gamma)
    by_taken = [spread(value) for value in steps_coef]
    by_change = [spread(value) for value in changes]

    def combine(t, carry):
        for plane in range(2):
            at = (plane, tile(8 * t))
            value = by_grad * grad[at]
            for i in range(pairs):
                value = value + by_taken[i] * taken[(i,) + at]
                value = value + by_change[i] * change[(i,) + at]
            direction[at] = value
        return carry

    lax.fori_loop(0, rows // 8, combine, 0)
    for copy in exchange:
        copy.wait_send()
    out.wait()


def on_device(
    n,
    field_now,
    field_before,
    lame_lambda,
    shear_modulus,
    density,
    source_field,
    wavelet,
    prior_mean,
    steps_taken,
    grad_change,
):
    comps, depth, rows, cols = field_now.shape
    pairs = steps_taken.shape[0]
    steps = wavelet.shape[0]
    size = chunk_rows(rows)
    chunks = rows // size
    f32 = jnp.float32
    state = pltpu.VMEM((comps, depth + 2, rows + 2 * PAD, cols), f32)
    model = pltpu.VMEM((depth, rows, cols), f32)
    stored = pltpu.VMEM((pairs, depth, rows, cols), f32)
    dma = pltpu.SemaphoreType.DMA
    anywhere = pl.BlockSpec(memory_space=pltpu.HBM)
    free = pl.BlockSpec(memory_space=pl.ANY)
    results = pl.pallas_call(
        functools.partial(kernel, n, steps, pairs, size),
        out_shape=(
            pltpu.VMEM(field_now.shape, f32),
            pltpu.VMEM(lame_lambda.shape, f32),
            pltpu.VMEM(lame_lambda.shape, f32),
        ),
        in_specs=[anywhere] * 6
        + [pl.BlockSpec(memory_space=pltpu.SMEM)]
        + [anywhere] * 3,
        out_specs=(pl.BlockSpec(memory_space=pltpu.VMEM),) * 3,
        scratch_shapes=[
            state,
            state,
            model,
            model,
            model,
            pltpu.VMEM((comps, depth, rows, cols), f32),
            model,
            stored,
            stored,
            pltpu.VMEM((2 * pairs, 8, 128), f32),
            pltpu.VMEM((1, 128), f32),
            pltpu.VMEM((n - 1, 1, 128), f32),
            dma((9,)),
            dma((1,)),
            dma((2, 2, chunks)),
            dma((2, 2, chunks)),
            dma((n - 1,)),
            dma((n - 1,)),
        ],
        compiler_params=pltpu.CompilerParams(
            collective_id=0, has_side_effects=True, vmem_limit_bytes=65000000
        ),
    )(
        field_now,
        field_before,
        lame_lambda,
        shear_modulus,
        density,
        source_field,
        wavelet,
        prior_mean,
        steps_taken,
        grad_change,
    )
    return pl.pallas_call(
        publish,
        out_shape=tuple(jax.ShapeDtypeStruct(value.shape, f32) for value in results),
        in_specs=[free] * 3,
        out_specs=(free, free, free),
        scratch_shapes=[dma((3,))],
        compiler_params=pltpu.CompilerParams(vmem_limit_bytes=1024 * 1024),
    )(*[pltpu.with_memory_space_constraint(value, pltpu.VMEM) for value in results])


def publish(*refs):
    sem = refs[-1]
    copies = [pltpu.make_async_copy(refs[i], refs[3 + i], sem.at[i]) for i in range(3)]
    for copy in copies:
        copy.start()
    for copy in copies:
        copy.wait()


def solution(mesh):
    n = mesh.shape["gz"]
    fields = P("sample", "gz", None, None)
    models = P("gz", "sample", None)
    placed = (
        fields,
        fields,
        models,
        models,
        models,
        fields,
        P("sample"),
        models,
        fields,
        fields,
    )
    return jax.shard_map(
        functools.partial(on_device, n),
        mesh=mesh,
        in_specs=placed,
        out_specs=(fields, models, models),
        check_vma=False,
    )
```

profile of v0, /device:TPU:0, one launch (start us, length us, event | category | flops | bytes accessed | tf_op | source)
XLA Modules:
  0.0 56.4 jit_solution(16692613304213532604)
XLA Ops:
  0.6 54.6 %shard_map.121 = (f32[3,2,160,256]{3,2,1,0:T(8,128)S(1)}, f32[2,160,256]{2,1,0:T(8,128)S(1)}, f32[2,160,256]{2,1,0:T(8,128)S(1)}) custom-call(f32[3,2,160,256]{3,2,1,0:T(8,128)} %now_hbm.1, f32[3,2,160,256]{3,2,1,0:T(8,128)} %before_hbm.1, f32[2,160,256]{2,1,0:T(8,128)} %lame_hbm.1, f32[2,160,256]{2,1,0:T(8,128)} %shear_hbm.1, f32[2,160,256]{2,1,0:T(8,128)} %density_hbm.1, ...), custom_call_target="tpu_custom_call" | custom-call | tf_op jit(solution)/shard_map/pallas_call | solution.py:461
  55.3 1.2 %shard_map.122 = (f32[3,2,160,256]{3,2,1,0:T(8,128)}, f32[2,160,256]{2,1,0:T(8,128)}, f32[2,160,256]{2,1,0:T(8,128)}) custom-call(f32[3,2,160,256]{3,2,1,0:T(8,128)S(1)} %get-tuple-element.6.refs_0_, f32[2,160,256]{2,1,0:T(8,128)S(1)} %get-tuple-element.7.refs_1_, f32[2,160,256]{2,1,0:T(8,128)S(1)} %get-tuple-element.8.refs_2_), custom_call_target="tpu_custom_call" | custom-call | tf_op jit(solution)/shard_map/pallas_call | solution.py:507
where the time goes:
time: 56.6 us; the launch traced here: 56.4 us
  Pallas kernels  55.8 us (99%)
  between operations  0.64 us (1%)
    pallas_call x1, Pallas kernels, on_device(): pl.pallas_call(functools.partial(kernel, n, steps, pairs, size), out_shap...  54.6 us
    pallas_call x1, Pallas kernels, on_device(): pl.pallas_call(publish, out_shape=tuple((jax.ShapeDtypeStruct(value.shape...  1.18 us

commit v1 on v0

v1 whole, which is shorter than its diff:
```python
import functools

import jax
import jax.numpy as jnp
from jax import lax
from jax.experimental import pallas as pl
from jax.experimental.pallas import tpu as pltpu
from jax.sharding import PartitionSpec as P

PAD = 8
CHUNK_ROWS = 32
PIECES = 4


def chunk_rows(rows):
    size = CHUNK_ROWS
    while rows % size:
        size //= 2
    return size


def tile(start):
    return pl.ds(pl.multiple_of(start, 8), 8)


def fold(value):
    out = value[:, 0:128]
    for k in range(1, value.shape[1] // 128):
        out = out + value[:, 128 * k : 128 * (k + 1)]
    return out


def whole(value):
    return jnp.sum(jnp.sum(value, axis=0, keepdims=True), axis=1, keepdims=True)


def product_pairs(pairs):
    found = [(i, pairs + j) for i in range(pairs) for j in range(pairs)]
    return found + [(pairs + i, pairs + j) for i in range(pairs) for j in range(i, pairs)]


def kernel(
    n,
    steps,
    pairs,
    size,
    now_hbm,
    before_hbm,
    lame_hbm,
    shear_hbm,
    density_hbm,
    source_hbm,
    wavelet_hbm,
    prior_hbm,
    taken_hbm,
    change_hbm,
    final,
    grad,
    taken,
    change,
    summed,
    even,
    odd,
    lame,
    shear,
    coeff,
    source,
    prior,
    wavelet,
    sums,
    part,
    gathered,
    load_sem,
    send_sem,
    recv_sem,
    part_sem,
):
    me = lax.axis_index("gz")
    rows, cols = lame.shape[1], lame.shape[2]
    chunks = rows // size
    tiles = size // 8
    has_low = me > 0
    has_high = me < n - 1
    inside = pl.ds(PAD, rows)
    chained = n - 1 <= steps

    barrier = pltpu.get_barrier_semaphore()

    def greet(device):
        pl.semaphore_signal(
            barrier, inc=1, device_id={"gz": device}, device_id_type=pl.DeviceIdType.MESH
        )

    if chained:

        @pl.when(has_low)
        def _():
            greet(me - 1)

        @pl.when(has_high)
        def _():
            greet(me + 1)

    else:
        for k in range(1, n):
            greet(lax.rem(me + k, n))

    loads = [
        pltpu.make_async_copy(src, dst, load_sem.at[i])
        for i, src, dst in (
            (
                0,
                now_hbm.at[:, :, pl.ds(0, size)],
                even.at[:, pl.ds(1, 2), pl.ds(PAD, size)],
            ),
            (
                1,
                now_hbm.at[:, :, pl.ds(size, rows - size)],
                even.at[:, pl.ds(1, 2), pl.ds(PAD + size, rows - size)],
            ),
            (2, lame_hbm, lame),
            (3, shear_hbm, shear),
            (4, density_hbm, coeff),
            (5, before_hbm, odd.at[:, pl.ds(1, 2), inside]),
            (6, source_hbm, source),
            (7, wavelet_hbm, wavelet),
            (8, taken_hbm, taken),
            (9, change_hbm, change),
            (10, prior_hbm, prior),
        )
    ]
    for load in loads:
        load.start()

    def rdma(ref, parity, up, where, sem):
        side = 0 if up else 1
        target = lax.rem(me + (1 if up else n - 1), n)
        return pltpu.make_async_remote_copy(
            src_ref=ref.at[:, 2 if up else 1, where],
            dst_ref=ref.at[:, 0 if up else 3, where],
            send_sem=send_sem.at[parity, side],
            recv_sem=sem,
            device_id={"gz": target},
            device_id_type=pl.DeviceIdType.MESH,
        )

    def halo(ref, parity, up, chunk):
        where = pl.ds(pl.multiple_of(PAD + chunk * size, 8), size)
        return rdma(ref, parity, up, where, recv_sem.at[parity, 0 if up else 1, chunk])

    def send(ref, parity, chunk):
        @pl.when(has_high)
        def _():
            halo(ref, parity, True, chunk).start()

        @pl.when(has_low)
        def _():
            halo(ref, parity, False, chunk).start()

    def sent(ref, parity):
        @pl.when(has_high)
        def _():
            rdma(ref, parity, True, inside, recv_sem.at[parity, 0, 0]).wait_send()

        @pl.when(has_low)
        def _():
            rdma(ref, parity, False, inside, recv_sem.at[parity, 1, 0]).wait_send()

    def received(ref, parity, chunk):
        @pl.when(has_low)
        def _():
            halo(ref, parity, True, chunk).wait_recv()

        @pl.when(has_high)
        def _():
            halo(ref, parity, False, chunk).wait_recv()

    loads[0].wait()
    if chained:
        pl.semaphore_wait(barrier, has_low.astype(jnp.int32) + has_high.astype(jnp.int32))
    else:
        pl.semaphore_wait(barrier, n - 1)

    send(even, 0, 0)
    loads[1].wait()

    def first(chunk, carry):
        send(even, 0, chunk)
        return carry

    lax.fori_loop(1, chunks, first, 0)

    edge = jnp.zeros((even.shape[0], 4, PAD, cols), jnp.float32)
    for ref in (even, odd):
        ref[:, :, pl.ds(0, PAD)] = edge
        ref[:, :, pl.ds(PAD + rows, PAD)] = edge

    def clear(plane):
        def body(t, carry):
            for ref in (even, odd):
                for comp in range(3):
                    ref[comp, plane, tile(PAD + 8 * t)] = jnp.zeros((8, cols), jnp.float32)
            return carry

        lax.fori_loop(0, rows // 8, body, 0)

    @pl.when(me == 0)
    def _():
        clear(0)

    @pl.when(me == n - 1)
    def _():
        clear(3)

    for load in loads[2:5]:
        load.wait()

    def prepare(t, carry):
        for plane in range(2):
            at = (plane, tile(8 * t))
            lame[at] = lame[at] + shear[at]
            coeff[at] = 0.04 / coeff[at]
            grad[at] = jnp.zeros((8, cols), jnp.float32)
        return carry

    lax.fori_loop(0, rows // 8, prepare, 0)
    for load in loads[5:]:
        load.wait()

    products = product_pairs(pairs)
    count = len(products)

    def stored(t, totals):
        totals = list(totals)
        for plane in range(2):
            vectors = [taken[i, plane, tile(8 * t)] for i in range(pairs)]
            vectors += [change[i, plane, tile(8 * t)] for i in range(pairs)]
            for k, (a, b) in enumerate(products):
                totals[k] = totals[k] + fold(vectors[a] * vectors[b])
        return tuple(totals)

    totals = lax.fori_loop(
        0, rows // 8, stored, tuple(jnp.zeros((8, 128), jnp.float32) for _ in products)
    )
    place = lax.broadcasted_iota(jnp.int32, (1, 128), 1)

    line = jnp.zeros((1, 128), jnp.float32)
    for k in range(count):
        line = jnp.where(place == k, whole(totals[k]), line)
    part[...] = line
    for i in range(2 * pairs):
        sums[i] = jnp.zeros((8, 128), jnp.float32)

    row_at = lax.broadcasted_iota(jnp.int32, (8, cols), 0)
    col_at = lax.broadcasted_iota(jnp.int32, (8, cols), 1)
    is_top, is_bottom = row_at == 0, row_at == 7
    is_left, is_right = col_at == 0, col_at == cols - 1

    def along_x(previous, value, following):
        minus = pltpu.roll(jnp.where(is_bottom, previous, value), 1, 0)
        plus = pltpu.roll(jnp.where(is_top, following, value), 7, 0)
        return minus, plus

    def along_y(value):
        minus = jnp.where(is_left, 0.0, pltpu.roll(value, 1, 1))
        plus = jnp.where(is_right, 0.0, pltpu.roll(value, cols - 1, 1))
        return minus, plus

    def delta_y(value):
        minus, plus = along_y(value)
        return plus - minus

    def correlate(current, t):
        def load(comp, plane, shift=0):
            return current[comp, plane, tile(PAD + 8 * (t + shift))]

        values = []
        for plane in range(2):
            low, mid, high = plane, plane + 1, plane + 2
            value = None
            for comp in range(3):
                centre = load(comp, mid)
                minus_x, plus_x = along_x(load(comp, mid, -1), centre, load(comp, mid, 1))
                minus_y, plus_y = along_y(centre)
                lap = (
                    (load(comp, high) + load(comp, low)) + (minus_x + plus_x)
                ) + ((minus_y + plus_y) - 6.0 * centre)
                value = centre * lap if value is None else value + centre * lap
            values.append(value)
        return values

    def update(step, current, other, t, last=False):
        amplitude = wavelet[step]

        def load(comp, plane, shift=0):
            return current[comp, plane, tile(PAD + 8 * (t + shift))]

        for plane in range(2):
            low, mid, high = plane, plane + 1, plane + 2
            at = tile(8 * t)
            here = tile(PAD + 8 * t)

            def delta_z(comp, shift=0):
                return load(comp, high, shift) - load(comp, low, shift)

            def delta_xz(comp, centre):
                minus, plus = along_x(delta_z(comp, -1), centre, delta_z(comp, 1))
                return plus - minus

            centre = [load(comp, mid) for comp in range(3)]
            diff = [delta_z(comp) for comp in range(3)]
            total = [load(comp, high) + load(comp, low) for comp in range(3)]
            xs = [along_x(load(comp, mid, -1), centre[comp], load(comp, mid, 1)) for comp in range(3)]
            ys = [along_y(centre[comp]) for comp in range(3)]
            sum_x = [minus + plus for minus, plus in xs]
            sum_y = [minus + plus for minus, plus in ys]
            dx = [plus - minus for minus, plus in xs]
            lap = [
                (total[comp] + sum_x[comp]) + (sum_y[comp] - 6.0 * centre[comp])
                for comp in range(3)
            ]
            mixed = [
                delta_xz(1, diff[1]) + delta_y(diff[2]),
                delta_xz(0, diff[0]) + delta_y(dx[2]),
                delta_y(diff[0] + dx[1]),
            ]
            own = [total[0], sum_x[1], sum_y[2]]
            both = lame[plane, at]
            mu = shear[plane, at]
            rate = coeff[plane, at]
            if not last:
                grad[plane, at] = grad[plane, at] + (
                    centre[0] * lap[0] + centre[1] * lap[1] + centre[2] * lap[2]
                )
            for comp in range(3):
                doubled = 2.0 * centre[comp]
                elastic = both * ((own[comp] - doubled) + 0.25 * mixed[comp]) + mu * lap[comp]
                value = (
                    doubled
                    - other[comp, mid, here]
                    + rate * (elastic + amplitude * source[comp, plane, at])
                )
                if last:
                    final[comp, plane, at] = value
                else:
                    other[comp, mid, here] = value

    def finish(current, t, totals):
        totals = list(totals)
        newest = correlate(current, t)
        for plane in range(2):
            at = (plane, tile(8 * t))
            value = (shear[at] - prior[at]) + 0.02 * (grad[at] + newest[plane])
            grad[at] = value
            for i in range(pairs):
                totals[i] = totals[i] + fold(taken[(i,) + at] * value)
                totals[pairs + i] = totals[pairs + i] + fold(change[(i,) + at] * value)
        return tuple(totals)

    def over_tiles(chunk, body):
        def tile_body(t, carry):
            body(chunk * tiles + t)
            return carry

        lax.fori_loop(0, tiles, tile_body, 0)

    def advance(step, current, other, parity):
        @pl.when(step > 0)
        def _():
            sent(other, 1 - parity)

        received(current, parity, 0)

        def chunk_body(chunk, carry):
            @pl.when(chunk + 1 < chunks)
            def _():
                received(current, parity, chunk + 1)

            over_tiles(chunk, lambda t: update(step, current, other, t))
            send(other, 1 - parity, chunk)
            return carry

        lax.fori_loop(0, chunks, chunk_body, 0)

    def two_steps(k, carry):
        advance(2 * k, even, odd, 0)
        advance(2 * k + 1, odd, even, 1)
        return carry

    lax.fori_loop(0, steps // 2 - 1, two_steps, 0)
    advance(steps - 2, even, odd, 0)

    def last_body(chunk, carry):
        received(odd, 1, chunk)
        totals = lax.fori_loop(
            chunk * tiles,
            chunk * tiles + tiles,
            functools.partial(finish, odd),
            tuple(sums[i] for i in range(2 * pairs)),
        )
        for i in range(2 * pairs):
            sums[i] = totals[i]

        @pl.when((chunk > 0) & (chunk < chunks - 1))
        def _():
            over_tiles(chunk - 1, lambda t: update(steps - 1, odd, even, t, True))

        return carry

    lax.fori_loop(0, chunks, last_body, 0)

    line = part[...]
    for i in range(2 * pairs):
        line = jnp.where(place == count + i, whole(sums[i]), line)
    part[...] = line

    def exchange(src, dst, target):
        return pltpu.make_async_remote_copy(
            src_ref=src,
            dst_ref=dst,
            send_sem=part_sem.at[0],
            recv_sem=part_sem.at[1],
            device_id={"gz": target},
            device_id_type=pl.DeviceIdType.MESH,
        )

    for k in range(1, n):
        exchange(part, gathered.at[k - 1], lax.rem(me + k, n)).start()

    for chunk in range(max(chunks - 2, 0), chunks):
        over_tiles(chunk, lambda t: update(steps - 1, odd, even, t, True))

    sent(even, 0)
    sent(odd, 1)
    everything = exchange(gathered, gathered, lax.rem(me + 1, n))
    everything.wait_recv()
    line = part[...]
    for k in range(n - 1):
        line = line + gathered[k]
    summed[...] = line
    everything.wait_send()


def publish(
    pairs,
    final,
    grad,
    taken,
    change,
    summed,
    final_hbm,
    grad_hbm,
    direction_hbm,
    direction,
    sem,
):
    rows, cols = grad.shape[1], grad.shape[2]
    copies = [
        pltpu.make_async_copy(final, final_hbm, sem.at[0]),
        pltpu.make_async_copy(grad, grad_hbm, sem.at[1]),
    ]
    for copy in copies:
        copy.start()

    place = lax.broadcasted_iota(jnp.int32, (1, 128), 1)
    products = product_pairs(pairs)
    count = len(products)
    where_of = {pair: k for k, pair in enumerate(products)}
    for i in range(2 * pairs):
        where_of[(i, 2 * pairs)] = count + i
    line = summed[...]
    cache = {}

    def inner(a, b):
        key = (min(a, b), max(a, b))
        if key not in cache:
            chosen = jnp.where(place == where_of[key], line, 0.0)
            cache[key] = jnp.sum(chosen, axis=1, keepdims=True)
        return cache[key]

    gradient_at = 2 * pairs
    curvature = [inner(i, pairs + i) for i in range(pairs)]
    alphas = [None] * pairs
    for i in reversed(range(pairs)):
        value = inner(i, gradient_at)
        for j in range(i + 1, pairs):
            value = value - alphas[j] * inner(i, pairs + j)
        alphas[i] = value / curvature[i]
    newest = 2 * pairs - 1
    gamma = curvature[pairs - 1] / inner(newest, newest)
    changes = [-gamma * alphas[i] for i in range(pairs)]
    steps_coef = [None] * pairs
    for i in range(pairs):
        value = gamma * inner(pairs + i, gradient_at)
        for j in range(pairs):
            value = value + changes[j] * inner(pairs + i, pairs + j)
        for j in range(i):
            value = value + steps_coef[j] * inner(j, pairs + i)
        steps_coef[i] = alphas[i] - value / curvature[i]

    def spread(value):
        return -jnp.broadcast_to(value, (8, cols))

    by_grad = spread(gamma)
    by_taken = [spread(value) for value in steps_coef]
    by_change = [spread(value) for value in changes]

    def combine(t, carry):
        for plane in range(2):
            at = (plane, tile(8 * t))
            value = by_grad * grad[at]
            for i in range(pairs):
                value = value + by_taken[i] * taken[(i,) + at]
                value = value + by_change[i] * change[(i,) + at]
            direction[at] = value
        return carry

    tiles = rows // 8
    pieces = PIECES
    while tiles % pieces:
        pieces -= 1
    for piece in range(pieces):
        first, count = piece * (tiles // pieces), tiles // pieces
        lax.fori_loop(first, first + count, combine, 0)
        span = pl.ds(8 * first, 8 * count)
        copy = pltpu.make_async_copy(
            direction.at[:, span], direction_hbm.at[:, span], sem.at[2 + piece]
        )
        copy.start()
        copies.append(copy)
    for copy in copies:
        copy.wait()


def on_device(
    n,
    field_now,
    field_before,
    lame_lambda,
    shear_modulus,
    density,
    source_field,
    wavelet,
    prior_mean,
    steps_taken,
    grad_change,
):
    comps, depth, rows, cols = field_now.shape
    pairs = steps_taken.shape[0]
    steps = wavelet.shape[0]
    size = chunk_rows(rows)
    chunks = rows // size
    f32 = jnp.float32
    state = pltpu.VMEM((comps, depth + 2, rows + 2 * PAD, cols), f32)
    model = pltpu.VMEM((depth, rows, cols), f32)
    dma = pltpu.SemaphoreType.DMA
    anywhere = pl.BlockSpec(memory_space=pltpu.HBM)
    free = pl.BlockSpec(memory_space=pl.ANY)
    in_vmem = pl.BlockSpec(memory_space=pltpu.VMEM)
    results = pl.pallas_call(
        functools.partial(kernel, n, steps, pairs, size),
        out_shape=(
            pltpu.VMEM(field_now.shape, f32),
            pltpu.VMEM(lame_lambda.shape, f32),
            pltpu.VMEM(steps_taken.shape, f32),
            pltpu.VMEM(grad_change.shape, f32),
            pltpu.VMEM((1, 128), f32),
        ),
        in_specs=[anywhere] * 10,
        out_specs=(in_vmem,) * 5,
        scratch_shapes=[
            state,
            state,
            model,
            model,
            model,
            pltpu.VMEM((comps, depth, rows, cols), f32),
            model,
            pltpu.SMEM((steps,), f32),
            pltpu.VMEM((2 * pairs, 8, 128), f32),
            pltpu.VMEM((1, 128), f32),
            pltpu.VMEM((n - 1, 1, 128), f32),
            dma((11,)),
            dma((2, 2)),
            dma((2, 2, chunks)),
            dma((2,)),
        ],
        compiler_params=pltpu.CompilerParams(
            collective_id=0, has_side_effects=True, vmem_limit_bytes=63000000
        ),
    )(
        field_now,
        field_before,
        lame_lambda,
        shear_modulus,
        density,
        source_field,
        wavelet,
        prior_mean,
        steps_taken,
        grad_change,
    )
    return pl.pallas_call(
        functools.partial(publish, pairs),
        out_shape=tuple(
            jax.ShapeDtypeStruct(shape, f32)
            for shape in (field_now.shape, lame_lambda.shape, lame_lambda.shape)
        ),
        in_specs=[in_vmem] * 5,
        out_specs=(free, free, free),
        scratch_shapes=[model, dma((2 + PIECES,))],
        compiler_params=pltpu.CompilerParams(vmem_limit_bytes=4 * 1024 * 1024),
    )(*[pltpu.with_memory_space_constraint(value, pltpu.VMEM) for value in results])


def solution(mesh):
    n = mesh.shape["gz"]
    fields = P("sample", "gz", None, None)
    models = P("gz", "sample", None)
    placed = (
        fields,
        fields,
        models,
        models,
        models,
        fields,
        P("sample"),
        models,
        fields,
        fields,
    )
    return jax.shard_map(
        functools.partial(on_device, n),
        mesh=mesh,
        in_specs=placed,
        out_specs=(fields, models, models),
        check_vma=False,
    )
```

time: 56.6 us -> 54.7 us (0.966)
  Pallas kernels: 55.8 us -> 53.9 us
    pallas_call x1, Pallas kernels: 54.6 us -> 52.7 us  [on_device(): pl.pallas_call(functools.partial(kernel, n, steps, pairs, size), out_shap...]
where the time goes in v1:
time: 54.7 us; the launch traced here: 54.5 us
  Pallas kernels  53.9 us (99%)
  between operations  0.64 us (1%)
    pallas_call x1, Pallas kernels, on_device(): pl.pallas_call(functools.partial(kernel, n, steps, pairs, size), out_shap...  52.7 us
    pallas_call x1, Pallas kernels, on_device(): pl.pallas_call(functools.partial(publish, pairs), out_shape=tuple((jax.Sh...  1.2 us

profile of v1, /device:TPU:0, one launch (start us, length us, event | category | flops | bytes accessed | tf_op | source)
XLA Modules:
  0.0 54.5 jit_solution(2771182677444683486)
XLA Ops:
  0.6 52.7 %shard_map.121 = (f32[3,2,160,256]{3,2,1,0:T(8,128)S(1)}, f32[2,160,256]{2,1,0:T(8,128)S(1)}, f32[4,2,160,256]{3,2,1,0:T(8,128)S(1)}, f32[4,2,160,256]{3,2,1,0:T(8,128)S(1)}, f32[1,128]{1,0:T(1,128)S(1)}) custom-call(f32[3,2,160,256]{3,2,1,0:T(8,128)} %now_hbm.1, f32[3,2,160,256]{3,2,1,0:T(8,128)} %before_hbm.1, f32[2,160,256]{2,1,0:T(8,128)} %lame_hbm.1, ...), custom_call_target="tpu_custom_call" | custom-call | tf_op jit(solution)/shard_map/pallas_call | solution.py:560
  53.3 1.2 %shard_map.122 = (f32[3,2,160,256]{3,2,1,0:T(8,128)}, f32[2,160,256]{2,1,0:T(8,128)}, f32[2,160,256]{2,1,0:T(8,128)}) custom-call(f32[3,2,160,256]{3,2,1,0:T(8,128)S(1)} %get-tuple-element.8.final, f32[2,160,256]{2,1,0:T(8,128)S(1)} %get-tuple-element.9.grad, f32[4,2,160,256]{3,2,1,0:T(8,128)S(1)} %get-tuple-element.10.taken, ...), custom_call_target="tpu_custom_call" | custom-call | tf_op jit(solution)/shard_map/pallas_call | solution.py:603

commit v2 on v1

--- a/solution.py
+++ b/solution.py
@@ -8,7 +8,7 @@
 from jax.sharding import PartitionSpec as P
 
 PAD = 8
-CHUNK_ROWS = 32
+CHUNK_ROWS = 16
 PIECES = 4
 
 
@@ -44,6 +44,7 @@
     steps,
     pairs,
     size,
+    relayed,
     now_hbm,
     before_hbm,
     lame_hbm,
@@ -56,33 +57,41 @@
     change_hbm,
     final,
     grad,
-    taken,
-    change,
+    pool,
     summed,
     even,
     odd,
-    lame,
-    shear,
-    coeff,
+    models,
     source,
-    prior,
     wavelet,
     sums,
     part,
     gathered,
+    product_out,
+    product_in,
     load_sem,
     send_sem,
-    recv_sem,
+    inner_sem,
+    outer_sem,
+    product_sem,
     part_sem,
 ):
     me = lax.axis_index("gz")
-    rows, cols = lame.shape[1], lame.shape[2]
+    rows, cols = grad.shape[1], grad.shape[2]
     chunks = rows // size
     tiles = size // 8
-    has_low = me > 0
-    has_high = me < n - 1
+    upper = lax.rem(me, 2)
+    has_outer = (me > 0) & (me < n - 1)
     inside = pl.ds(PAD, rows)
     chained = n - 1 <= steps
+    inner_target = me + 1 - 2 * upper
+    outer_target = lax.rem(me + n - 1 + 2 * upper, n)
+    inner_plane, outer_plane = 2 - upper, 1 + upper
+    inner_halo, outer_halo = 3 - 3 * upper, 3 * upper
+    early = relayed * upper
+    late = relayed - early
+    lame, shear, coeff, prior = (models.at[i] for i in range(4))
+    taken, change = pool.at[pl.ds(0, pairs)], pool.at[pl.ds(pairs, pairs)]
 
     barrier = pltpu.get_barrier_semaphore()
 
@@ -93,14 +102,11 @@
 
     if chained:
 
-        @pl.when(has_low)
-        def _():
-            greet(me - 1)
-
-        @pl.when(has_high)
-        def _():
-            greet(me + 1)
-
+        @pl.when(has_outer)
+        def _():
+            greet(outer_target)
+
+        greet(inner_target)
     else:
         for k in range(1, n):
             greet(lax.rem(me + k, n))
@@ -119,65 +125,85 @@
                 even.at[:, pl.ds(1, 2), pl.ds(PAD + size, rows - size)],
             ),
             (2, lame_hbm, lame),
-            (3, shear_hbm, shear),
-            (4, density_hbm, coeff),
-            (5, before_hbm, odd.at[:, pl.ds(1, 2), inside]),
-            (6, source_hbm, source),
-            (7, wavelet_hbm, wavelet),
-            (8, taken_hbm, taken),
-            (9, change_hbm, change),
-            (10, prior_hbm, prior),
+            (2, shear_hbm, shear),
+            (2, density_hbm, coeff),
+            (2, prior_hbm, prior),
+            (3, before_hbm, odd.at[:, pl.ds(1, 2), inside]),
+            (4, source_hbm, source),
+            (5, wavelet_hbm, wavelet),
+            (6, taken_hbm, taken),
+            (6, change_hbm, change),
         )
     ]
     for load in loads:
         load.start()
 
-    def rdma(ref, parity, up, where, sem):
-        side = 0 if up else 1
-        target = lax.rem(me + (1 if up else n - 1), n)
+    def remote(src, dst, send, recv, target):
         return pltpu.make_async_remote_copy(
-            src_ref=ref.at[:, 2 if up else 1, where],
-            dst_ref=ref.at[:, 0 if up else 3, where],
-            send_sem=send_sem.at[parity, side],
-            recv_sem=sem,
+            src_ref=src,
+            dst_ref=dst,
+            send_sem=send,
+            recv_sem=recv,
             device_id={"gz": target},
             device_id_type=pl.DeviceIdType.MESH,
         )
 
-    def halo(ref, parity, up, chunk):
-        where = pl.ds(pl.multiple_of(PAD + chunk * size, 8), size)
-        return rdma(ref, parity, up, where, recv_sem.at[parity, 0 if up else 1, chunk])
+    def span(chunk):
+        return pl.ds(pl.multiple_of(PAD + chunk * size, 8), size)
+
+    def send_inner(ref, parity, chunk):
+        remote(
+            ref.at[:, inner_plane, span(chunk)],
+            ref.at[:, 3 * upper, span(chunk)],
+            send_sem.at[parity],
+            inner_sem.at[parity],
+            inner_target,
+        ).start()
+
+    def send_outer(ref, parity, chunk):
+        remote(
+            ref.at[:, outer_plane, span(chunk)],
+            ref.at[:, 3 - 3 * upper, span(chunk)],
+            send_sem.at[parity],
+            outer_sem.at[parity, chunk],
+            outer_target,
+        ).start()
 
     def send(ref, parity, chunk):
-        @pl.when(has_high)
-        def _():
-            halo(ref, parity, True, chunk).start()
-
-        @pl.when(has_low)
-        def _():
-            halo(ref, parity, False, chunk).start()
+        @pl.when(has_outer)
+        def _():
+            send_outer(ref, parity, chunk)
+
+        send_inner(ref, parity, chunk)
 
     def sent(ref, parity):
-        @pl.when(has_high)
-        def _():
-            rdma(ref, parity, True, inside, recv_sem.at[parity, 0, 0]).wait_send()
-
-        @pl.when(has_low)
-        def _():
-            rdma(ref, parity, False, inside, recv_sem.at[parity, 1, 0]).wait_send()
-
-    def received(ref, parity, chunk):
-        @pl.when(has_low)
-        def _():
-            halo(ref, parity, True, chunk).wait_recv()
-
-        @pl.when(has_high)
-        def _():
-            halo(ref, parity, False, chunk).wait_recv()
+        def wait(planes):
+            whole_planes = ref.at[:, planes, inside]
+            remote(
+                whole_planes, whole_planes, send_sem.at[parity], inner_sem.at[parity], inner_target
+            ).wait_send()
+
+        @pl.when(has_outer)
+        def _():
+            wait(pl.ds(1, 2))
+
+        @pl.when(jnp.logical_not(has_outer))
+        def _():
+            wait(pl.ds(1, 1))
+
+    def received_inner(ref, parity):
+        halo = ref.at[:, inner_halo, inside]
+        remote(halo, halo, send_sem.at[parity], inner_sem.at[parity], inner_target).wait_recv()
+
+    def received_outer(ref, parity, chunk):
+        halo = ref.at[:, outer_halo, span(chunk)]
+        remote(
+            halo, halo, send_sem.at[parity], outer_sem.at[parity, chunk], outer_target
+        ).wait_recv()
 
     loads[0].wait()
     if chained:
-        pl.semaphore_wait(barrier, has_low.astype(jnp.int32) + has_high.astype(jnp.int32))
+        pl.semaphore_wait(barrier, 1 + has_outer.astype(jnp.int32))
     else:
         pl.semaphore_wait(barrier, n - 1)
 
@@ -195,25 +221,17 @@
         ref[:, :, pl.ds(0, PAD)] = edge
         ref[:, :, pl.ds(PAD + rows, PAD)] = edge
 
-    def clear(plane):
+    @pl.when(jnp.logical_not(has_outer))
+    def _():
         def body(t, carry):
             for ref in (even, odd):
                 for comp in range(3):
-                    ref[comp, plane, tile(PAD + 8 * t)] = jnp.zeros((8, cols), jnp.float32)
+                    ref[comp, outer_halo, tile(PAD + 8 * t)] = jnp.zeros((8, cols), jnp.float32)
             return carry
 
         lax.fori_loop(0, rows // 8, body, 0)
 
-    @pl.when(me == 0)
-    def _():
-        clear(0)
-
-    @pl.when(me == n - 1)
-    def _():
-        clear(3)
-
-    for load in loads[2:5]:
-        load.wait()
+    pltpu.make_async_copy(models, models, load_sem.at[2]).wait()
 
     def prepare(t, carry):
         for plane in range(2):
@@ -224,8 +242,9 @@
         return carry
 
     lax.fori_loop(0, rows // 8, prepare, 0)
-    for load in loads[5:]:
+    for load in loads[6:9]:
         load.wait()
+    pltpu.make_async_copy(pool, pool, load_sem.at[6]).wait()
 
     products = product_pairs(pairs)
     count = len(products)
@@ -233,8 +252,7 @@
     def stored(t, totals):
         totals = list(totals)
         for plane in range(2):
-            vectors = [taken[i, plane, tile(8 * t)] for i in range(pairs)]
-            vectors += [change[i, plane, tile(8 * t)] for i in range(pairs)]
+            vectors = [pool[i, plane, tile(8 * t)] for i in range(2 * pairs)]
             for k, (a, b) in enumerate(products):
                 totals[k] = totals[k] + fold(vectors[a] * vectors[b])
         return tuple(totals)
@@ -248,8 +266,6 @@
     for k in range(count):
         line = jnp.where(place == k, whole(totals[k]), line)
     part[...] = line
-    for i in range(2 * pairs):
-        sums[i] = jnp.zeros((8, 128), jnp.float32)
 
     row_at = lax.broadcasted_iota(jnp.int32, (8, cols), 0)
     col_at = lax.broadcasted_iota(jnp.int32, (8, cols), 1)
@@ -269,25 +285,6 @@
     def delta_y(value):
         minus, plus = along_y(value)
         return plus - minus
-
-    def correlate(current, t):
-        def load(comp, plane, shift=0):
-            return current[comp, plane, tile(PAD + 8 * (t + shift))]
-
-        values = []
-        for plane in range(2):
-            low, mid, high = plane, plane + 1, plane + 2
-            value = None
-            for comp in range(3):
-                centre = load(comp, mid)
-                minus_x, plus_x = along_x(load(comp, mid, -1), centre, load(comp, mid, 1))
-                minus_y, plus_y = along_y(centre)
-                lap = (
-                    (load(comp, high) + load(comp, low)) + (minus_x + plus_x)
-                ) + ((minus_y + plus_y) - 6.0 * centre)
-                value = centre * lap if value is None else value + centre * lap
-            values.append(value)
-        return values
 
     def update(step, current, other, t, last=False):
         amplitude = wavelet[step]
@@ -345,18 +342,6 @@
                 else:
                     other[comp, mid, here] = value
 
-    def finish(current, t, totals):
-        totals = list(totals)
-        newest = correlate(current, t)
-        for plane in range(2):
-            at = (plane, tile(8 * t))
-            value = (shear[at] - prior[at]) + 0.02 * (grad[at] + newest[plane])
-            grad[at] = value
-            for i in range(pairs):
-                totals[i] = totals[i] + fold(taken[(i,) + at] * value)
-                totals[pairs + i] = totals[pairs + i] + fold(change[(i,) + at] * value)
-        return tuple(totals)
-
     def over_tiles(chunk, body):
         def tile_body(t, carry):
             body(chunk * tiles + t)
@@ -364,50 +349,151 @@
 
         lax.fori_loop(0, tiles, tile_body, 0)
 
-    def advance(step, current, other, parity):
+    def wait_outer(ref, parity, chunk):
+        @pl.when(has_outer)
+        def _():
+            received_outer(ref, parity, chunk)
+
+    def advance(step, current, other, parity, relay):
         @pl.when(step > 0)
         def _():
             sent(other, 1 - parity)
 
-        received(current, parity, 0)
+        received_inner(current, parity)
+        wait_outer(current, parity, 0)
 
         def chunk_body(chunk, carry):
             @pl.when(chunk + 1 < chunks)
             def _():
-                received(current, parity, chunk + 1)
+                wait_outer(current, parity, chunk + 1)
 
             over_tiles(chunk, lambda t: update(step, current, other, t))
-            send(other, 1 - parity, chunk)
+            if relay:
+
+                @pl.when(has_outer & ((chunk < early) | (chunk >= early + relayed)))
+                def _():
+                    send_outer(other, 1 - parity, chunk)
+
+                send_inner(other, 1 - parity, chunk)
+            else:
+                send(other, 1 - parity, chunk)
             return carry
 
         lax.fori_loop(0, chunks, chunk_body, 0)
 
     def two_steps(k, carry):
-        advance(2 * k, even, odd, 0)
-        advance(2 * k + 1, odd, even, 1)
+        advance(2 * k, even, odd, 0, False)
+        advance(2 * k + 1, odd, even, 1, False)
         return carry
 
     lax.fori_loop(0, steps // 2 - 1, two_steps, 0)
-    advance(steps - 2, even, odd, 0)
-
-    def last_body(chunk, carry):
-        received(odd, 1, chunk)
-        totals = lax.fori_loop(
-            chunk * tiles,
-            chunk * tiles + tiles,
-            functools.partial(finish, odd),
-            tuple(sums[i] for i in range(2 * pairs)),
+    advance(steps - 2, even, odd, 0, True)
+
+    def across(t):
+        here = tile(PAD + 8 * t)
+        value = odd[0, outer_plane, here] * odd[0, outer_halo, here]
+        for comp in range(1, 3):
+            value = value + odd[comp, outer_plane, here] * odd[comp, outer_halo, here]
+        return value
+
+    returned = remote(
+        product_out, product_in, product_sem.at[0], product_sem.at[1], outer_target
+    )
+    if relayed:
+
+        @pl.when(has_outer)
+        def _():
+            def multiply(chunk, carry):
+                received_outer(odd, 1, early + chunk)
+
+                def body(t, inner):
+                    product_out[tile(8 * t)] = across(early * tiles + t)
+                    return inner
+
+                lax.fori_loop(chunk * tiles, chunk * tiles + tiles, body, 0)
+                return carry
+
+            lax.fori_loop(0, relayed, multiply, 0)
+            returned.start()
+
+            def follow(chunk, carry):
+                send_outer(odd, 1, early + chunk)
+                return carry
+
+            lax.fori_loop(0, relayed, follow, 0)
+
+    received_inner(odd, 1)
+
+    def weigh(totals, at, value):
+        return tuple(
+            totals[i] + fold(pool[(i,) + at] * value) for i in range(2 * pairs)
         )
+
+    def own_part(t, totals):
+        def load(comp, plane, shift=0):
+            return odd[comp, plane, tile(PAD + 8 * (t + shift))]
+
+        for mid, around in ((inner_plane, (outer_plane, inner_halo)), (outer_plane, (inner_plane,))):
+            at = (mid - 1, tile(8 * t))
+            value = None
+            for comp in range(3):
+                centre = load(comp, mid)
+                minus_x, plus_x = along_x(load(comp, mid, -1), centre, load(comp, mid, 1))
+                minus_y, plus_y = along_y(centre)
+                total = load(comp, around[0])
+                for plane in around[1:]:
+                    total = total + load(comp, plane)
+                lap = (total + (minus_x + plus_x)) + ((minus_y + plus_y) - 6.0 * centre)
+                value = centre * lap if value is None else value + centre * lap
+            value = (shear[at] - prior[at]) + 0.02 * (grad[at] + value)
+            grad[at] = value
+            totals = weigh(totals, at, value)
+        return totals
+
+    totals = lax.fori_loop(
+        0,
+        rows // 8,
+        own_part,
+        tuple(jnp.zeros((8, 128), jnp.float32) for _ in range(2 * pairs)),
+    )
+    for i in range(2 * pairs):
+        sums[i] = totals[i]
+
+    @pl.when(has_outer)
+    def _():
+        def add(product):
+            def body(t, totals):
+                at = (outer_plane - 1, tile(8 * t))
+                value = 0.02 * product(t)
+                grad[at] = grad[at] + value
+                return weigh(totals, at, value)
+
+            return body
+
+        totals = tuple(sums[i] for i in range(2 * pairs))
+        if relayed:
+            totals = lax.fori_loop(
+                early * tiles,
+                (early + relayed) * tiles,
+                add(lambda t: product_out[tile(8 * (t - early * tiles))]),
+                totals,
+            )
+
+        def direct(chunk, totals):
+            received_outer(odd, 1, chunk)
+            return lax.fori_loop(chunk * tiles, chunk * tiles + tiles, add(across), totals)
+
+        totals = lax.fori_loop(2 * relayed, chunks, direct, totals)
+        if relayed:
+            returned.wait_recv()
+            totals = lax.fori_loop(
+                late * tiles,
+                (late + relayed) * tiles,
+                add(lambda t: product_in[tile(8 * (t - late * tiles))]),
+                totals,
+            )
         for i in range(2 * pairs):
             sums[i] = totals[i]
-
-        @pl.when((chunk > 0) & (chunk < chunks - 1))
-        def _():
-            over_tiles(chunk - 1, lambda t: update(steps - 1, odd, even, t, True))
-
-        return carry
-
-    lax.fori_loop(0, chunks, last_body, 0)
 
     line = part[...]
     for i in range(2 * pairs):
@@ -415,24 +501,36 @@
     part[...] = line
 
     def exchange(src, dst, target):
-        return pltpu.make_async_remote_copy(
-            src_ref=src,
-            dst_ref=dst,
-            send_sem=part_sem.at[0],
-            recv_sem=part_sem.at[1],
-            device_id={"gz": target},
-            device_id_type=pl.DeviceIdType.MESH,
-        )
+        return remote(src, dst, part_sem.at[0], part_sem.at[1], target)
 
     for k in range(1, n):
         exchange(part, gathered.at[k - 1], lax.rem(me + k, n)).start()
 
-    for chunk in range(max(chunks - 2, 0), chunks):
+    def close(chunk, carry):
         over_tiles(chunk, lambda t: update(steps - 1, odd, even, t, True))
+        return carry
+
+    ready = min(2 * relayed + 1, chunks) if relayed else 0
+    lax.fori_loop(ready, chunks, close, 0)
+    if relayed:
+
+        @pl.when(has_outer)
+        def _():
+            def arrive(chunk, carry):
+                received_outer(odd, 1, late + chunk)
+                return carry
+
+            lax.fori_loop(0, relayed, arrive, 0)
+
+        lax.fori_loop(0, ready, close, 0)
+
+        @pl.when(has_outer)
+        def _():
+            returned.wait_send()
 
     sent(even, 0)
     sent(odd, 1)
-    everything = exchange(gathered, gathered, lax.rem(me + 1, n))
+    everything = exchange(gathered, gathered, inner_target)
     everything.wait_recv()
     line = part[...]
     for k in range(n - 1):
@@ -445,8 +543,7 @@
     pairs,
     final,
     grad,
-    taken,
-    change,
+    pool,
     summed,
     final_hbm,
     grad_hbm,
@@ -510,8 +607,8 @@
             at = (plane, tile(8 * t))
             value = by_grad * grad[at]
             for i in range(pairs):
-                value = value + by_taken[i] * taken[(i,) + at]
-                value = value + by_change[i] * change[(i,) + at]
+                value = value + by_taken[i] * pool[(i,) + at]
+                value = value + by_change[i] * pool[(pairs + i,) + at]
             direction[at] = value
         return carry
 
@@ -521,7 +618,7 @@
         pieces -= 1
     for piece in range(pieces):
         first, count = piece * (tiles // pieces), tiles // pieces
-        lax.fori_loop(first, first + count, combine, 0)
+        lax.fori_loop(first, first + count, combine, 0, unroll=True)
         span = pl.ds(8 * first, 8 * count)
         copy = pltpu.make_async_copy(
             direction.at[:, span], direction_hbm.at[:, span], sem.at[2 + piece]
@@ -550,39 +647,41 @@
     steps = wavelet.shape[0]
     size = chunk_rows(rows)
     chunks = rows // size
+    relayed = 3 * chunks // 10
     f32 = jnp.float32
     state = pltpu.VMEM((comps, depth + 2, rows + 2 * PAD, cols), f32)
     model = pltpu.VMEM((depth, rows, cols), f32)
+    returned = pltpu.VMEM((max(relayed, 1) * size, cols), f32)
     dma = pltpu.SemaphoreType.DMA
     anywhere = pl.BlockSpec(memory_space=pltpu.HBM)
     free = pl.BlockSpec(memory_space=pl.ANY)
     in_vmem = pl.BlockSpec(memory_space=pltpu.VMEM)
     results = pl.pallas_call(
-        functools.partial(kernel, n, steps, pairs, size),
+        functools.partial(kernel, n, steps, pairs, size, relayed),
         out_shape=(
             pltpu.VMEM(field_now.shape, f32),
             pltpu.VMEM(lame_lambda.shape, f32),
-            pltpu.VMEM(steps_taken.shape, f32),
-            pltpu.VMEM(grad_change.shape, f32),
+            pltpu.VMEM((2 * pairs,) + lame_lambda.shape, f32),
             pltpu.VMEM((1, 128), f32),
         ),
         in_specs=[anywhere] * 10,
-        out_specs=(in_vmem,) * 5,
+        out_specs=(in_vmem,) * 4,
         scratch_shapes=[
             state,
             state,
-            model,
-            model,
-            model,
+            pltpu.VMEM((4, depth, rows, cols), f32),
             pltpu.VMEM((comps, depth, rows, cols), f32),
-            model,
             pltpu.SMEM((steps,), f32),
             pltpu.VMEM((2 * pairs, 8, 128), f32),
             pltpu.VMEM((1, 128), f32),
             pltpu.VMEM((n - 1, 1, 128), f32),
-            dma((11,)),
-            dma((2, 2)),
-            dma((2, 2, chunks)),
+            returned,
+            returned,
+            dma((7,)),
+            dma((2,)),
+            dma((2,)),
+            dma((2, chunks)),
+            dma((2,)),
             dma((2,)),
         ],
         compiler_params=pltpu.CompilerParams(
@@ -606,7 +705,7 @@
             jax.ShapeDtypeStruct(shape, f32)
             for shape in (field_now.shape, lame_lambda.shape, lame_lambda.shape)
         ),
-        in_specs=[in_vmem] * 5,
+        in_specs=[in_vmem] * 4,
         out_specs=(free, free, free),
         scratch_shapes=[model, dma((2 + PIECES,))],
         compiler_params=pltpu.CompilerParams(vmem_limit_bytes=4 * 1024 * 1024),

time: 54.7 us -> 53.6 us (0.980)
  Pallas kernels: 53.9 us -> 52.8 us
    pallas_call x1, Pallas kernels: 52.7 us -> 51.6 us  [on_device(): pl.pallas_call(functools.partial(kernel, n, steps, pairs, size, relayed),...]
where the time goes in v2:
time: 53.6 us; the launch traced here: 53.4 us
  Pallas kernels  52.8 us (99%)
  between operations  0.64 us (1%)
    pallas_call x1, Pallas kernels, on_device(): pl.pallas_call(functools.partial(kernel, n, steps, pairs, size, relayed),...  51.6 us
    pallas_call x1, Pallas kernels, on_device(): pl.pallas_call(functools.partial(publish, pairs), out_shape=tuple((jax.Sh...  1.2 us

profile of v2, /device:TPU:0, one launch (start us, length us, event | category | flops | bytes accessed | tf_op | source)
XLA Modules:
  0.0 53.4 jit_solution(7875838398451563241)
XLA Ops:
  0.6 51.6 %shard_map.121 = (f32[3,2,160,256]{3,2,1,0:T(8,128)S(1)}, f32[2,160,256]{2,1,0:T(8,128)S(1)}, f32[8,2,160,256]{3,2,1,0:T(8,128)S(1)}, f32[1,128]{1,0:T(1,128)S(1)}) custom-call(f32[3,2,160,256]{3,2,1,0:T(8,128)} %now_hbm.1, f32[3,2,160,256]{3,2,1,0:T(8,128)} %before_hbm.1, f32[2,160,256]{2,1,0:T(8,128)} %lame_hbm.1, f32[2,160,256]{2,1,0:T(8,128)} %shear_hbm.1, ...), custom_call_target="tpu_custom_call" | custom-call | tf_op jit(solution)/shard_map/pallas_call | solution.py:659
  52.2 1.2 %shard_map.122 = (f32[3,2,160,256]{3,2,1,0:T(8,128)}, f32[2,160,256]{2,1,0:T(8,128)}, f32[2,160,256]{2,1,0:T(8,128)}) custom-call(f32[3,2,160,256]{3,2,1,0:T(8,128)S(1)} %get-tuple-element.7.final, f32[2,160,256]{2,1,0:T(8,128)S(1)} %get-tuple-element.8.grad, f32[8,2,160,256]{3,2,1,0:T(8,128)S(1)} %get-tuple-element.9.pool, ...), custom_call_target="tpu_custom_call" | custom-call | tf_op jit(solution)/shard_map/pallas_call | solution.py:702

commit v3 on v2

--- a/solution.py
+++ b/solution.py
@@ -69,7 +69,6 @@
     gathered,
     product_out,
     product_in,
-    load_sem,
     send_sem,
     inner_sem,
     outer_sem,
@@ -112,27 +111,27 @@
             greet(lax.rem(me + k, n))
 
     loads = [
-        pltpu.make_async_copy(src, dst, load_sem.at[i])
-        for i, src, dst in (
+        pltpu.make_async_copy(src, dst, sem)
+        for sem, src, dst in (
             (
-                0,
+                outer_sem.at[1, 0],
                 now_hbm.at[:, :, pl.ds(0, size)],
                 even.at[:, pl.ds(1, 2), pl.ds(PAD, size)],
             ),
             (
-                1,
+                inner_sem.at[1],
                 now_hbm.at[:, :, pl.ds(size, rows - size)],
                 even.at[:, pl.ds(1, 2), pl.ds(PAD + size, rows - size)],
             ),
-            (2, lame_hbm, lame),
-            (2, shear_hbm, shear),
-            (2, density_hbm, coeff),
-            (2, prior_hbm, prior),
-            (3, before_hbm, odd.at[:, pl.ds(1, 2), inside]),
-            (4, source_hbm, source),
-            (5, wavelet_hbm, wavelet),
-            (6, taken_hbm, taken),
-            (6, change_hbm, change),
+            (product_sem.at[0], lame_hbm, lame),
+            (product_sem.at[0], shear_hbm, shear),
+            (product_sem.at[0], density_hbm, coeff),
+            (product_sem.at[0], prior_hbm, prior),
+            (product_sem.at[1], before_hbm, odd.at[:, pl.ds(1, 2), inside]),
+            (part_sem.at[0], source_hbm, source),
+            (send_sem.at[1], wavelet_hbm, wavelet),
+            (part_sem.at[1], taken_hbm, taken),
+            (part_sem.at[1], change_hbm, change),
         )
     ]
     for load in loads:
@@ -231,7 +230,7 @@
 
         lax.fori_loop(0, rows // 8, body, 0)
 
-    pltpu.make_async_copy(models, models, load_sem.at[2]).wait()
+    pltpu.make_async_copy(models, models, product_sem.at[0]).wait()
 
     def prepare(t, carry):
         for plane in range(2):
@@ -244,7 +243,7 @@
     lax.fori_loop(0, rows // 8, prepare, 0)
     for load in loads[6:9]:
         load.wait()
-    pltpu.make_async_copy(pool, pool, load_sem.at[6]).wait()
+    pltpu.make_async_copy(pool, pool, part_sem.at[1]).wait()
 
     products = product_pairs(pairs)
     count = len(products)
@@ -396,25 +395,32 @@
             value = value + odd[comp, outer_plane, here] * odd[comp, outer_halo, here]
         return value
 
-    returned = remote(
-        product_out, product_in, product_sem.at[0], product_sem.at[1], outer_target
-    )
-    if relayed:
+    def returned(first, number, sem):
+        where = pl.ds(first * size, number * size)
+        return remote(
+            product_out.at[where],
+            product_in.at[where],
+            product_sem.at[0],
+            product_sem.at[sem],
+            outer_target,
+        )
+
+    pieces = [(0, relayed - 1, 1), (relayed - 1, 1, 2)] if relayed > 1 else [(0, relayed, 1)]
+    pieces = [piece for piece in pieces if piece[1]]
+    if pieces:
 
         @pl.when(has_outer)
         def _():
             def multiply(chunk, carry):
                 received_outer(odd, 1, early + chunk)
-
-                def body(t, inner):
+                for k in range(tiles):
+                    t = chunk * tiles + k
                     product_out[tile(8 * t)] = across(early * tiles + t)
-                    return inner
-
-                lax.fori_loop(chunk * tiles, chunk * tiles + tiles, body, 0)
                 return carry
 
-            lax.fori_loop(0, relayed, multiply, 0)
-            returned.start()
+            for piece in pieces:
+                lax.fori_loop(piece[0], piece[0] + piece[1], multiply, 0)
+                returned(*piece).start()
 
             def follow(chunk, carry):
                 send_outer(odd, 1, early + chunk)
@@ -455,42 +461,42 @@
         rows // 8,
         own_part,
         tuple(jnp.zeros((8, 128), jnp.float32) for _ in range(2 * pairs)),
+        unroll=2,
     )
     for i in range(2 * pairs):
         sums[i] = totals[i]
 
     @pl.when(has_outer)
     def _():
-        def add(product):
-            def body(t, totals):
-                at = (outer_plane - 1, tile(8 * t))
-                value = 0.02 * product(t)
-                grad[at] = grad[at] + value
-                return weigh(totals, at, value)
-
-            return body
+        def add(t, product, totals):
+            at = (outer_plane - 1, tile(8 * t))
+            value = 0.02 * product
+            grad[at] = grad[at] + value
+            return weigh(totals, at, value)
+
+        def added(products, start):
+            return lambda t, totals: add(start * tiles + t, products[tile(8 * t)], totals)
 
         totals = tuple(sums[i] for i in range(2 * pairs))
         if relayed:
-            totals = lax.fori_loop(
-                early * tiles,
-                (early + relayed) * tiles,
-                add(lambda t: product_out[tile(8 * (t - early * tiles))]),
-                totals,
-            )
+            totals = lax.fori_loop(0, relayed * tiles, added(product_out, early), totals)
 
         def direct(chunk, totals):
             received_outer(odd, 1, chunk)
-            return lax.fori_loop(chunk * tiles, chunk * tiles + tiles, add(across), totals)
+            for k in range(tiles):
+                t = chunk * tiles + k
+                totals = add(t, across(t), totals)
+            return totals
 
         totals = lax.fori_loop(2 * relayed, chunks, direct, totals)
-        if relayed:
-            returned.wait_recv()
+        for piece in pieces:
+            returned(*piece).wait_recv()
             totals = lax.fori_loop(
-                late * tiles,
-                (late + relayed) * tiles,
-                add(lambda t: product_in[tile(8 * (t - late * tiles))]),
+                piece[0] * tiles,
+                (piece[0] + piece[1]) * tiles,
+                added(product_in, late),
                 totals,
+                unroll=tiles,
             )
         for i in range(2 * pairs):
             sums[i] = totals[i]
@@ -503,8 +509,13 @@
     def exchange(src, dst, target):
         return remote(src, dst, part_sem.at[0], part_sem.at[1], target)
 
-    for k in range(1, n):
-        exchange(part, gathered.at[k - 1], lax.rem(me + k, n)).start()
+    for target in range(n):
+
+        @pl.when(me != target)
+        def _():
+            exchange(part, gathered.at[me], target).start()
+
+    gathered[me] = line
 
     def close(chunk, carry):
         over_tiles(chunk, lambda t: update(steps - 1, odd, even, t, True))
@@ -526,14 +537,15 @@
 
         @pl.when(has_outer)
         def _():
-            returned.wait_send()
+            returned(0, relayed, 1).wait_send()
 
     sent(even, 0)
     sent(odd, 1)
-    everything = exchange(gathered, gathered, inner_target)
+    others = gathered.at[pl.ds(0, n - 1)]
+    everything = exchange(others, others, inner_target)
     everything.wait_recv()
-    line = part[...]
-    for k in range(n - 1):
+    line = gathered[0]
+    for k in range(1, n):
         line = line + gathered[k]
     summed[...] = line
     everything.wait_send()
@@ -674,14 +686,13 @@
             pltpu.SMEM((steps,), f32),
             pltpu.VMEM((2 * pairs, 8, 128), f32),
             pltpu.VMEM((1, 128), f32),
-            pltpu.VMEM((n - 1, 1, 128), f32),
+            pltpu.VMEM((n, 1, 128), f32),
             returned,
             returned,
-            dma((7,)),
             dma((2,)),
             dma((2,)),
             dma((2, chunks)),
-            dma((2,)),
+            dma((3,)),
             dma((2,)),
         ],
         compiler_params=pltpu.CompilerParams(

time: 53.6 us -> 53.2 us (level)
  no operation moved by 1% of the time
where the time goes in v3:
time: 53.2 us; the launch traced here: 53 us
  Pallas kernels  52.4 us (98%)
  between operations  0.64 us (1%)
    pallas_call x1, Pallas kernels, on_device(): pl.pallas_call(functools.partial(kernel, n, steps, pairs, size, relayed),...  51.2 us
    pallas_call x1, Pallas kernels, on_device(): pl.pallas_call(functools.partial(publish, pairs), out_shape=tuple((jax.Sh...  1.2 us

profile of v3, /device:TPU:0, one launch (start us, length us, event | category | flops | bytes accessed | tf_op | source)
XLA Modules:
  0.0 53.0 jit_solution(9436850569266494106)
XLA Ops:
  0.6 51.2 %shard_map.121 = (f32[3,2,160,256]{3,2,1,0:T(8,128)S(1)}, f32[2,160,256]{2,1,0:T(8,128)S(1)}, f32[8,2,160,256]{3,2,1,0:T(8,128)S(1)}, f32[1,128]{1,0:T(1,128)S(1)}) custom-call(f32[3,2,160,256]{3,2,1,0:T(8,128)} %now_hbm.1, f32[3,2,160,256]{3,2,1,0:T(8,128)} %before_hbm.1, f32[2,160,256]{2,1,0:T(8,128)} %lame_hbm.1, f32[2,160,256]{2,1,0:T(8,128)} %shear_hbm.1, ...), custom_call_target="tpu_custom_call" | custom-call | tf_op jit(solution)/shard_map/pallas_call | solution.py:671
  51.8 1.2 %shard_map.122 = (f32[3,2,160,256]{3,2,1,0:T(8,128)}, f32[2,160,256]{2,1,0:T(8,128)}, f32[2,160,256]{2,1,0:T(8,128)}) custom-call(f32[3,2,160,256]{3,2,1,0:T(8,128)S(1)} %get-tuple-element.7.final, f32[2,160,256]{2,1,0:T(8,128)S(1)} %get-tuple-element.8.grad, f32[8,2,160,256]{3,2,1,0:T(8,128)S(1)} %get-tuple-element.9.pool, ...), custom_call_target="tpu_custom_call" | custom-call | tf_op jit(solution)/shard_map/pallas_call | solution.py:713

commit v4 on v3

--- a/solution.py
+++ b/solution.py
@@ -10,6 +10,7 @@
 PAD = 8
 CHUNK_ROWS = 16
 PIECES = 4
+RELAY_AT = 1
 
 
 def chunk_rows(rows):
@@ -45,6 +46,7 @@
     pairs,
     size,
     relayed,
+    helpers,
     now_hbm,
     before_hbm,
     lame_hbm,
@@ -69,11 +71,14 @@
     gathered,
     product_out,
     product_in,
+    detour,
     send_sem,
     inner_sem,
     outer_sem,
     product_sem,
     part_sem,
+    detour_sem,
+    ready,
 ):
     me = lax.axis_index("gz")
     rows, cols = grad.shape[1], grad.shape[2]
@@ -92,6 +97,14 @@
     lame, shear, coeff, prior = (models.at[i] for i in range(4))
     taken, change = pool.at[pl.ds(0, pairs)], pool.at[pl.ds(pairs, pairs)]
 
+    sample = lax.axis_index("sample")
+    below, above = n - 3, n - 2
+    assisted = (sample == 0) & ((me == below) | (me == above))
+    helping = (sample >= 1) & (sample <= helpers)
+    carries = helping & ((me == below - 1) | (me == above + 1))
+    stripped = chunks - 1
+    strip = pl.ds(PAD + stripped * size, size)
+
     barrier = pltpu.get_barrier_semaphore()
 
     def greet(device):
@@ -99,6 +112,14 @@
             barrier, inc=1, device_id={"gz": device}, device_id_type=pl.DeviceIdType.MESH
         )
 
+    def greet_across(semaphore, target_sample, device):
+        pl.semaphore_signal(
+            semaphore,
+            inc=1,
+            device_id={"sample": target_sample, "gz": device},
+            device_id_type=pl.DeviceIdType.MESH,
+        )
+
     if chained:
 
         @pl.when(has_outer)
@@ -106,6 +127,13 @@
             greet(outer_target)
 
         greet(inner_target)
+        if helpers:
+
+            @pl.when(assisted)
+            def _():
+                for helper in range(1, helpers + 1):
+                    greet_across(barrier, helper, inner_target)
+
     else:
         for k in range(1, n):
             greet(lax.rem(me + k, n))
@@ -137,13 +165,16 @@
     for load in loads:
         load.start()
 
-    def remote(src, dst, send, recv, target):
+    def remote(src, dst, send, recv, target, target_sample=None):
+        device = {"gz": target}
+        if target_sample is not None:
+            device["sample"] = target_sample
         return pltpu.make_async_remote_copy(
             src_ref=src,
             dst_ref=dst,
             send_sem=send,
             recv_sem=recv,
-            device_id={"gz": target},
+            device_id=device,
             device_id_type=pl.DeviceIdType.MESH,
         )
 
@@ -168,8 +199,40 @@
             outer_target,
         ).start()
 
+    def send_strips(ref, parity):
+        for helper in range(1, helpers + 1):
+            remote(
+                ref.at[helper - 1, outer_plane, strip],
+                detour.at[parity],
+                send_sem.at[parity],
+                detour_sem.at[parity],
+                inner_target,
+                helper,
+            ).start()
+
+    def pass_on(ref, parity):
+        return remote(
+            detour.at[parity],
+            ref.at[sample - 1, 3 * upper, strip],
+            part_sem.at[0],
+            detour_sem.at[parity],
+            me + 2 - 4 * upper,
+            0,
+        )
+
+    def received_strips(ref, parity):
+        strips = ref.at[:, outer_halo, strip]
+        remote(strips, strips, send_sem.at[parity], detour_sem.at[parity], outer_target).wait_recv()
+
     def send(ref, parity, chunk):
         @pl.when(has_outer)
+        def _():
+            send_outer(ref, parity, chunk)
+
+        send_inner(ref, parity, chunk)
+
+    def send_but_strips(ref, parity, chunk):
+        @pl.when(has_outer & jnp.logical_not(assisted & (chunk >= stripped)))
         def _():
             send_outer(ref, parity, chunk)
 
@@ -200,17 +263,26 @@
             halo, halo, send_sem.at[parity], outer_sem.at[parity, chunk], outer_target
         ).wait_recv()
 
-    loads[0].wait()
     if chained:
-        pl.semaphore_wait(barrier, 1 + has_outer.astype(jnp.int32))
+        expected = 1 + has_outer.astype(jnp.int32)
+        if helpers:
+            expected = expected + carries.astype(jnp.int32)
+        pl.semaphore_wait(barrier, expected)
     else:
         pl.semaphore_wait(barrier, n - 1)
 
+    if helpers:
+
+        @pl.when(carries)
+        def _():
+            greet_across(ready, 0, me + 1 - 2 * upper)
+
+    loads[0].wait()
     send(even, 0, 0)
     loads[1].wait()
 
     def first(chunk, carry):
-        send(even, 0, chunk)
+        (send_but_strips if helpers else send)(even, 0, chunk)
         return carry
 
     lax.fori_loop(1, chunks, first, 0)
@@ -229,6 +301,13 @@
             return carry
 
         lax.fori_loop(0, rows // 8, body, 0)
+
+    if helpers:
+
+        @pl.when(assisted)
+        def _():
+            pl.semaphore_wait(ready, helpers)
+            send_strips(even, 0)
 
     pltpu.make_async_copy(models, models, product_sem.at[0]).wait()
 
@@ -353,7 +432,16 @@
         def _():
             received_outer(ref, parity, chunk)
 
-    def advance(step, current, other, parity, relay):
+    def wait_all_but_strips(ref, parity, chunk):
+        @pl.when(assisted & (chunk == stripped))
+        def _():
+            received_strips(ref, parity)
+
+        @pl.when(has_outer & jnp.logical_not(assisted & (chunk >= stripped)))
+        def _():
+            received_outer(ref, parity, chunk)
+
+    def advance(step, current, other, parity, relay, detours=False):
         @pl.when(step > 0)
         def _():
             sent(other, 1 - parity)
@@ -364,7 +452,17 @@
         def chunk_body(chunk, carry):
             @pl.when(chunk + 1 < chunks)
             def _():
-                wait_outer(current, parity, chunk + 1)
+                (wait_all_but_strips if detours else wait_outer)(current, parity, chunk + 1)
+
+            if detours:
+
+                @pl.when(carries & (chunk == RELAY_AT))
+                def _():
+                    received = detour.at[parity]
+                    remote(
+                        received, received, part_sem.at[0], detour_sem.at[parity], inner_target
+                    ).wait_recv()
+                    pass_on(current, parity).start()
 
             over_tiles(chunk, lambda t: update(step, current, other, t))
             if relay:
@@ -385,7 +483,16 @@
         advance(2 * k + 1, odd, even, 1, False)
         return carry
 
-    lax.fori_loop(0, steps // 2 - 1, two_steps, 0)
+    if helpers:
+        advance(0, even, odd, 0, False, True)
+
+        @pl.when(carries)
+        def _():
+            pass_on(even, 0).wait_send()
+
+        advance(1, odd, even, 1, False)
+
+    lax.fori_loop(1 if helpers else 0, steps // 2 - 1, two_steps, 0)
     advance(steps - 2, even, odd, 0, True)
 
     def across(t):
@@ -643,6 +750,7 @@
 
 def on_device(
     n,
+    samples,
     field_now,
     field_before,
     lame_lambda,
@@ -660,6 +768,8 @@
     size = chunk_rows(rows)
     chunks = rows // size
     relayed = 3 * chunks // 10
+    assist = samples > comps and 8 <= n <= steps + 1 and steps >= 6 and chunks > 4
+    helpers = comps if assist else 0
     f32 = jnp.float32
     state = pltpu.VMEM((comps, depth + 2, rows + 2 * PAD, cols), f32)
     model = pltpu.VMEM((depth, rows, cols), f32)
@@ -669,7 +779,7 @@
     free = pl.BlockSpec(memory_space=pl.ANY)
     in_vmem = pl.BlockSpec(memory_space=pltpu.VMEM)
     results = pl.pallas_call(
-        functools.partial(kernel, n, steps, pairs, size, relayed),
+        functools.partial(kernel, n, steps, pairs, size, relayed, helpers),
         out_shape=(
             pltpu.VMEM(field_now.shape, f32),
             pltpu.VMEM(lame_lambda.shape, f32),
@@ -689,11 +799,14 @@
             pltpu.VMEM((n, 1, 128), f32),
             returned,
             returned,
+            pltpu.VMEM((1, size, cols), f32),
             dma((2,)),
             dma((2,)),
             dma((2, chunks)),
             dma((3,)),
             dma((2,)),
+            dma((1,)),
+            pltpu.SemaphoreType.REGULAR,
         ],
         compiler_params=pltpu.CompilerParams(
             collective_id=0, has_side_effects=True, vmem_limit_bytes=63000000
@@ -740,7 +853,7 @@
         fields,
     )
     return jax.shard_map(
-        functools.partial(on_device, n),
+        functools.partial(on_device, n, mesh.shape["sample"]),
         mesh=mesh,
         in_specs=placed,
         out_specs=(fields, models, models),

time: 53.2 us -> 52.7 us (level)
  no operation moved by 1% of the time
where the time goes in v4:
time: 52.7 us; the launch traced here: 52.5 us
  Pallas kernels  51.9 us (98%)
  between operations  0.64 us (1%)
    pallas_call x1, Pallas kernels, on_device(): pl.pallas_call(functools.partial(kernel, n, steps, pairs, size, relayed,...  50.7 us
    pallas_call x1, Pallas kernels, on_device(): pl.pallas_call(functools.partial(publish, pairs), out_shape=tuple((jax.Sh...  1.2 us

profile of v4, /device:TPU:0, one launch (start us, length us, event | category | flops | bytes accessed | tf_op | source)
XLA Modules:
  0.0 52.5 jit_solution(11140540054477121370)
XLA Ops:
  0.6 50.7 %shard_map.121 = (f32[3,2,160,256]{3,2,1,0:T(8,128)S(1)}, f32[2,160,256]{2,1,0:T(8,128)S(1)}, f32[8,2,160,256]{3,2,1,0:T(8,128)S(1)}, f32[1,128]{1,0:T(1,128)S(1)}) custom-call(f32[3,2,160,256]{3,2,1,0:T(8,128)} %now_hbm.1, f32[3,2,160,256]{3,2,1,0:T(8,128)} %before_hbm.1, f32[2,160,256]{2,1,0:T(8,128)} %lame_hbm.1, f32[2,160,256]{2,1,0:T(8,128)} %shear_hbm.1, ...), custom_call_target="tpu_custom_call" | custom-call | tf_op jit(solution)/shard_map/pallas_call | solution.py:781
  51.3 1.2 %shard_map.122 = (f32[3,2,160,256]{3,2,1,0:T(8,128)}, f32[2,160,256]{2,1,0:T(8,128)}, f32[2,160,256]{2,1,0:T(8,128)}) custom-call(f32[3,2,160,256]{3,2,1,0:T(8,128)S(1)} %get-tuple-element.7.final, f32[2,160,256]{2,1,0:T(8,128)S(1)} %get-tuple-element.8.grad, f32[8,2,160,256]{3,2,1,0:T(8,128)S(1)} %get-tuple-element.9.pool, ...), custom_call_target="tpu_custom_call" | custom-call | tf_op jit(solution)/shard_map/pallas_call | solution.py:826

commit v5 on v4

--- a/solution.py
+++ b/solution.py
@@ -102,8 +102,8 @@
     assisted = (sample == 0) & ((me == below) | (me == above))
     helping = (sample >= 1) & (sample <= helpers)
     carries = helping & ((me == below - 1) | (me == above + 1))
-    stripped = chunks - 1
-    strip = pl.ds(PAD + stripped * size, size)
+    stripped = chunks - 2
+    strip = pl.ds(PAD + stripped * size, 2 * size)
 
     barrier = pltpu.get_barrier_semaphore()
 
@@ -221,7 +221,7 @@
         )
 
     def received_strips(ref, parity):
-        strips = ref.at[:, outer_halo, strip]
+        strips = ref.at[pl.ds(0, helpers), outer_halo, strip]
         remote(strips, strips, send_sem.at[parity], detour_sem.at[parity], outer_target).wait_recv()
 
     def send(ref, parity, chunk):
@@ -231,10 +231,24 @@
 
         send_inner(ref, parity, chunk)
 
+    others = pl.ds(helpers, even.shape[0] - helpers)
+
     def send_but_strips(ref, parity, chunk):
-        @pl.when(has_outer & jnp.logical_not(assisted & (chunk >= stripped)))
+        cut = assisted & (chunk >= stripped)
+
+        @pl.when(has_outer & jnp.logical_not(cut))
         def _():
             send_outer(ref, parity, chunk)
+
+        @pl.when(cut)
+        def _():
+            remote(
+                ref.at[others, outer_plane, span(chunk)],
+                ref.at[others, 3 - 3 * upper, span(chunk)],
+                send_sem.at[parity],
+                outer_sem.at[parity, chunk],
+                outer_target,
+            ).start()
 
         send_inner(ref, parity, chunk)
 
@@ -441,6 +455,13 @@
         def _():
             received_outer(ref, parity, chunk)
 
+        @pl.when(assisted & (chunk >= stripped))
+        def _():
+            rest = ref.at[others, outer_halo, span(chunk)]
+            remote(
+                rest, rest, send_sem.at[parity], outer_sem.at[parity, chunk], outer_target
+            ).wait_recv()
+
     def advance(step, current, other, parity, relay, detours=False):
         @pl.when(step > 0)
         def _():
@@ -628,8 +649,10 @@
         over_tiles(chunk, lambda t: update(steps - 1, odd, even, t, True))
         return carry
 
-    ready = min(2 * relayed + 1, chunks) if relayed else 0
-    lax.fori_loop(ready, chunks, close, 0)
+    if relayed > 1:
+        lax.fori_loop(2 * relayed + 1, chunks, close, 0)
+        after = upper * (relayed + 1)
+        lax.fori_loop(after, relayed - 1 + upper * (relayed + 2), close, 0)
     if relayed:
 
         @pl.when(has_outer)
@@ -640,7 +663,12 @@
 
             lax.fori_loop(0, relayed, arrive, 0)
 
-        lax.fori_loop(0, ready, close, 0)
+    if relayed > 1:
+        before = (1 - upper) * (relayed - 1)
+        lax.fori_loop(before, 2 * relayed + 1 - upper * relayed, close, 0)
+    else:
+        lax.fori_loop(0, chunks, close, 0)
+    if relayed:
 
         @pl.when(has_outer)
         def _():
@@ -648,8 +676,8 @@
 
     sent(even, 0)
     sent(odd, 1)
-    others = gathered.at[pl.ds(0, n - 1)]
-    everything = exchange(others, others, inner_target)
+    arriving = gathered.at[pl.ds(0, n - 1)]
+    everything = exchange(arriving, arriving, inner_target)
     everything.wait_recv()
     line = gathered[0]
     for k in range(1, n):
@@ -769,7 +797,7 @@
     chunks = rows // size
     relayed = 3 * chunks // 10
     assist = samples > comps and 8 <= n <= steps + 1 and steps >= 6 and chunks > 4
-    helpers = comps if assist else 0
+    helpers = comps - 1 if assist else 0
     f32 = jnp.float32
     state = pltpu.VMEM((comps, depth + 2, rows + 2 * PAD, cols), f32)
     model = pltpu.VMEM((depth, rows, cols), f32)
@@ -799,7 +827,7 @@
             pltpu.VMEM((n, 1, 128), f32),
             returned,
             returned,
-            pltpu.VMEM((1, size, cols), f32),
+            pltpu.VMEM((1, 2 * size, cols), f32),
             dma((2,)),
             dma((2,)),
             dma((2, chunks)),

time: 52.7 us -> 52.5 us (level)
  no operation moved by 1% of the time
where the time goes in v5:
time: 52.5 us; the launch traced here: 52.4 us
  Pallas kernels  51.7 us (98%)
  between operations  0.64 us (1%)
    pallas_call x1, Pallas kernels, on_device(): pl.pallas_call(functools.partial(kernel, n, steps, pairs, size, relayed,...  50.5 us
    pallas_call x1, Pallas kernels, on_device(): pl.pallas_call(functools.partial(publish, pairs), out_shape=tuple((jax.Sh...  1.2 us

profile of v5, /device:TPU:0, one launch (start us, length us, event | category | flops | bytes accessed | tf_op | source)
XLA Modules:
  0.0 52.4 jit_solution(7125825482395281279)
XLA Ops:
  0.6 50.5 %shard_map.121 = (f32[3,2,160,256]{3,2,1,0:T(8,128)S(1)}, f32[2,160,256]{2,1,0:T(8,128)S(1)}, f32[8,2,160,256]{3,2,1,0:T(8,128)S(1)}, f32[1,128]{1,0:T(1,128)S(1)}) custom-call(f32[3,2,160,256]{3,2,1,0:T(8,128)} %now_hbm.1, f32[3,2,160,256]{3,2,1,0:T(8,128)} %before_hbm.1, f32[2,160,256]{2,1,0:T(8,128)} %lame_hbm.1, f32[2,160,256]{2,1,0:T(8,128)} %shear_hbm.1, ...), custom_call_target="tpu_custom_call" | custom-call | tf_op jit(solution)/shard_map/pallas_call | solution.py:809
  51.2 1.2 %shard_map.122 = (f32[3,2,160,256]{3,2,1,0:T(8,128)}, f32[2,160,256]{2,1,0:T(8,128)}, f32[2,160,256]{2,1,0:T(8,128)}) custom-call(f32[3,2,160,256]{3,2,1,0:T(8,128)S(1)} %get-tuple-element.7.final, f32[2,160,256]{2,1,0:T(8,128)S(1)} %get-tuple-element.8.grad, f32[8,2,160,256]{3,2,1,0:T(8,128)S(1)} %get-tuple-element.9.pool, ...), custom_call_target="tpu_custom_call" | custom-call | tf_op jit(solution)/shard_map/pallas_call | solution.py:854

commit v6 on v5

--- a/solution.py
+++ b/solution.py
@@ -10,7 +10,7 @@
 PAD = 8
 CHUNK_ROWS = 16
 PIECES = 4
-RELAY_AT = 1
+RELAY_AT = 0
 
 
 def chunk_rows(rows):
@@ -102,8 +102,8 @@
     assisted = (sample == 0) & ((me == below) | (me == above))
     helping = (sample >= 1) & (sample <= helpers)
     carries = helping & ((me == below - 1) | (me == above + 1))
-    stripped = chunks - 2
-    strip = pl.ds(PAD + stripped * size, 2 * size)
+    stripped = chunks - 3
+    strip = pl.ds(PAD + stripped * size, 3 * size)
 
     barrier = pltpu.get_barrier_semaphore()
 
@@ -827,7 +827,7 @@
             pltpu.VMEM((n, 1, 128), f32),
             returned,
             returned,
-            pltpu.VMEM((1, 2 * size, cols), f32),
+            pltpu.VMEM((1, 3 * size, cols), f32),
             dma((2,)),
             dma((2,)),
             dma((2, chunks)),

time: 52.5 us -> 52.3 us (level)
  no operation moved by 1% of the time
where the time goes in v6:
time: 52.3 us; the launch traced here: 52 us
  Pallas kernels  51.4 us (98%)
  between operations  0.64 us (1%)
    pallas_call x1, Pallas kernels, on_device(): pl.pallas_call(functools.partial(kernel, n, steps, pairs, size, relayed,...  50.2 us
    pallas_call x1, Pallas kernels, on_device(): pl.pallas_call(functools.partial(publish, pairs), out_shape=tuple((jax.Sh...  1.2 us

profile of v6, /device:TPU:0, one launch (start us, length us, event | category | flops | bytes accessed | tf_op | source)
XLA Modules:
  0.0 52.0 jit_solution(13345022026451617578)
XLA Ops:
  0.6 50.2 %shard_map.121 = (f32[3,2,160,256]{3,2,1,0:T(8,128)S(1)}, f32[2,160,256]{2,1,0:T(8,128)S(1)}, f32[8,2,160,256]{3,2,1,0:T(8,128)S(1)}, f32[1,128]{1,0:T(1,128)S(1)}) custom-call(f32[3,2,160,256]{3,2,1,0:T(8,128)} %now_hbm.1, f32[3,2,160,256]{3,2,1,0:T(8,128)} %before_hbm.1, f32[2,160,256]{2,1,0:T(8,128)} %lame_hbm.1, f32[2,160,256]{2,1,0:T(8,128)} %shear_hbm.1, ...), custom_call_target="tpu_custom_call" | custom-call | tf_op jit(solution)/shard_map/pallas_call | solution.py:809
  50.8 1.2 %shard_map.122 = (f32[3,2,160,256]{3,2,1,0:T(8,128)}, f32[2,160,256]{2,1,0:T(8,128)}, f32[2,160,256]{2,1,0:T(8,128)}) custom-call(f32[3,2,160,256]{3,2,1,0:T(8,128)S(1)} %get-tuple-element.7.final, f32[2,160,256]{2,1,0:T(8,128)S(1)} %get-tuple-element.8.grad, f32[8,2,160,256]{3,2,1,0:T(8,128)S(1)} %get-tuple-element.9.pool, ...), custom_call_target="tpu_custom_call" | custom-call | tf_op jit(solution)/shard_map/pallas_call | solution.py:854

commit v7 on v5

--- a/solution.py
+++ b/solution.py
@@ -10,7 +10,7 @@
 PAD = 8
 CHUNK_ROWS = 16
 PIECES = 4
-RELAY_AT = 1
+RELAY_AT = 0
 
 
 def chunk_rows(rows):
@@ -301,6 +301,13 @@
 
     lax.fori_loop(1, chunks, first, 0)
 
+    if helpers:
+
+        @pl.when(assisted)
+        def _():
+            pl.semaphore_wait(ready, helpers)
+            send_strips(even, 0)
+
     edge = jnp.zeros((even.shape[0], 4, PAD, cols), jnp.float32)
     for ref in (even, odd):
         ref[:, :, pl.ds(0, PAD)] = edge
@@ -315,13 +322,6 @@
             return carry
 
         lax.fori_loop(0, rows // 8, body, 0)
-
-    if helpers:
-
-        @pl.when(assisted)
-        def _():
-            pl.semaphore_wait(ready, helpers)
-            send_strips(even, 0)
 
     pltpu.make_async_copy(models, models, product_sem.at[0]).wait()
 

time: 52.5 us -> 52.5 us (level)
  no operation moved by 1% of the time
where the time goes in v7:
time: 52.5 us; the launch traced here: 52.4 us
  Pallas kernels  51.7 us (98%)
  between operations  0.64 us (1%)
    pallas_call x1, Pallas kernels, on_device(): pl.pallas_call(functools.partial(kernel, n, steps, pairs, size, relayed,...  50.5 us
    pallas_call x1, Pallas kernels, on_device(): pl.pallas_call(functools.partial(publish, pairs), out_shape=tuple((jax.Sh...  1.2 us

profile of v7, /device:TPU:0, one launch (start us, length us, event | category | flops | bytes accessed | tf_op | source)
XLA Modules:
  0.0 52.4 jit_solution(17726698382585739310)
XLA Ops:
  0.6 50.5 %shard_map.121 = (f32[3,2,160,256]{3,2,1,0:T(8,128)S(1)}, f32[2,160,256]{2,1,0:T(8,128)S(1)}, f32[8,2,160,256]{3,2,1,0:T(8,128)S(1)}, f32[1,128]{1,0:T(1,128)S(1)}) custom-call(f32[3,2,160,256]{3,2,1,0:T(8,128)} %now_hbm.1, f32[3,2,160,256]{3,2,1,0:T(8,128)} %before_hbm.1, f32[2,160,256]{2,1,0:T(8,128)} %lame_hbm.1, f32[2,160,256]{2,1,0:T(8,128)} %shear_hbm.1, ...), custom_call_target="tpu_custom_call" | custom-call | tf_op jit(solution)/shard_map/pallas_call | solution.py:809
  51.2 1.2 %shard_map.122 = (f32[3,2,160,256]{3,2,1,0:T(8,128)}, f32[2,160,256]{2,1,0:T(8,128)}, f32[2,160,256]{2,1,0:T(8,128)}) custom-call(f32[3,2,160,256]{3,2,1,0:T(8,128)S(1)} %get-tuple-element.7.final, f32[2,160,256]{2,1,0:T(8,128)S(1)} %get-tuple-element.8.grad, f32[8,2,160,256]{3,2,1,0:T(8,128)S(1)} %get-tuple-element.9.pool, ...), custom_call_target="tpu_custom_call" | custom-call | tf_op jit(solution)/shard_map/pallas_call | solution.py:854
